TPU v7x, 128 devices: a whole 4x4x4 slice. The times are simulated.
128 devices in a mesh: lat: 8 (over y, core), lon: 16 (over z, x).
Axes of the slice: x: 4, y: 4, z: 4, core: 2. Of those that a mesh axis runs over, the one named last changes fastest.
Arguments:
- grid_in: bfloat16 [262144, 227], P(('lat', 'lon')), may hold values from -6 to 6
- mesh_emb: bfloat16 [65536, 512], P(('lat', 'lon')), may hold values from -6 to 6
- enc_dest: int32 [262144, 2], P(('lat', 'lon')), may hold values from 0 to 127, as said below
- enc_node: int32 [262144, 2], P(('lat', 'lon')), may hold values from 0 to 511
- enc_dist: float32 [262144, 2], P(('lat', 'lon')), may hold values from 0.2 to 2
- dec_dist: float32 [262144, 2], P(('lat', 'lon')), may hold values from 0.2 to 2
- mesh_src: int32 [65536, 8], P(('lat', 'lon')), may hold values from 0 to 65535, as said below
- proc_dist: float32 [65536, 8], P(('lat', 'lon')), may hold values from 0.2 to 2
- w_grid_in: bfloat16 [227, 512], replicated, may hold values from -0.375 to 0.375
- w_enc_src: bfloat16 [512, 512], replicated, may hold values from -0.25 to 0.25
- w_enc_dist: float32 [512], replicated, may hold values from -6 to 6
- w_mesh_self: bfloat16 [512, 512], replicated, may hold values from -0.25 to 0.25
- w_mesh_agg: bfloat16 [512, 512], replicated, may hold values from -0.09375 to 0.09375
- w_proc_send: bfloat16 [512, 512], replicated, may hold values from -0.25 to 0.25
- w_proc_recv: bfloat16 [512, 512], replicated, may hold values from -0.25 to 0.25
- w_proc_dist: float32 [512], replicated, may hold values from -6 to 6
- w_proc_self: bfloat16 [512, 512], replicated, may hold values from -0.25 to 0.25
- w_proc_agg: bfloat16 [512, 512], replicated, may hold values from -0.125 to 0.125
- w_dec_send: bfloat16 [512, 512], replicated, may hold values from -0.25 to 0.25
- w_dec_recv: bfloat16 [512, 512], replicated, may hold values from -0.25 to 0.25
- w_dec_dist: float32 [512], replicated, may hold values from -6 to 6
- w_grid_self: bfloat16 [512, 512], replicated, may hold values from -0.25 to 0.25
- w_grid_agg: bfloat16 [512, 512], replicated, may hold values from -0.1875 to 0.1875
- w_grid_out: bfloat16 [512, 227], replicated, may hold values from -0.25 to 0.25
Outputs:
- pred: bfloat16 [262144, 227], P(('lat', 'lon'))
Inputs may be any that keep to these rules, and one draw needn't show every extreme that they name: `enc_dest`: patch p lies at patch row p // 16 and column p % 16; cell c lies on the device of index c // 2048 (lat index times 16 plus lon index). The first entry of a row is the cell's own patch. The second is a different patch whose row differs by at most one (no wrap) and whose column differs by at most one, columns wrapping around. Among the cells of one device, no patch is named in the second entry by more than 512 cells, and some patch by exactly 512. `mesh_src`: node n lies in patch n // 512. Every sender lies in the receiver's patch or in one whose row differs by at most one (no wrap) and whose column differs by at most one, columns wrapping around.
All inputs are finite; a program needn't handle non-finite values.
Results may differ from a plain program's by a relative error of at most 0.014.
Values may be sent and summed in bfloat16 or wider, within the bound.
A program may use at most 128 MiB of HBM per device.

v0:
```python
import jax
import jax.numpy as jnp
from jax import lax
from jax.sharding import PartitionSpec as P


def shifted(shard, axis, by):
    peers = lax.axis_size(axis)
    pairs = [(i, i + by) for i in range(peers) if 0 <= i + by < peers]
    return lax.ppermute(shard, axis, pairs)


def passed_along(block, axis, distance):
    devices = range(lax.axis_size(axis))
    route = [((i - distance) % len(devices), i) for i in devices]
    return lax.ppermute(block, axis, route)


def with_halo(shard, sides, width):
    for axis, dim in sides:
        peers, length = (lax.axis_size(axis), shard.shape[dim])
        up = [(i, (i + 1) % peers) for i in range(peers)]
        down = [(j, i) for i, j in up]
        last = lax.slice_in_dim(shard, length - width, length, axis=dim)
        leading = lax.slice_in_dim(shard, 0, width, axis=dim)
        before = lax.ppermute(last, axis, up)
        after = lax.ppermute(leading, axis, down)
        shard = jnp.concatenate([before, shard, after], axis=dim)
    return shard


def neighbour_index(global_ids, mesh_rows, n_lon, my_lat, my_lon):
    source_patch = global_ids // mesh_rows
    source_node = global_ids % mesh_rows
    step_row = source_patch // n_lon - my_lat + 1
    step_col = (source_patch % n_lon - my_lon + 1 + n_lon) % n_lon
    return (step_row * 3 + step_col) * mesh_rows + source_node


def shards(
    grid_in,
    mesh_emb,
    enc_dest,
    enc_node,
    enc_dist,
    dec_dist,
    mesh_src,
    proc_dist,
    w_grid_in,
    w_enc_src,
    w_enc_dist,
    w_mesh_self,
    w_mesh_agg,
    w_proc_send,
    w_proc_recv,
    w_proc_dist,
    w_proc_self,
    w_proc_agg,
    w_dec_send,
    w_dec_recv,
    w_dec_dist,
    w_grid_self,
    w_grid_agg,
    w_grid_out,
):
    n_lon = lax.axis_size("lon")
    cells = grid_in.shape[0]
    width = w_grid_in.shape[1]
    mesh_rows = mesh_emb.shape[0]
    degree = mesh_src.shape[1]
    my_lat = lax.axis_index("lat")
    my_lon = lax.axis_index("lon")
    grid_h = jax.nn.silu(jnp.dot(grid_in, w_grid_in, preferred_element_type=jnp.float32)).astype(
        jnp.bfloat16
    )
    enc_proj = jnp.dot(grid_h, w_enc_src, preferred_element_type=jnp.float32)
    messages = jax.nn.silu(enc_proj[:, None, :] + enc_dist[:, :, None] * w_enc_dist).astype(
        jnp.bfloat16
    )
    own_select = (
        enc_node[:, 0][None, :] == jnp.arange(mesh_rows, dtype=jnp.int32)[:, None]
    ).astype(jnp.bfloat16)
    own_part = jnp.dot(own_select, messages[:, 0, :], preferred_element_type=jnp.float32)
    far_key = neighbour_index(
        enc_dest[:, 1] * mesh_rows + enc_node[:, 1], mesh_rows, n_lon, my_lat, my_lon
    )
    far_select = (far_key[None, :] == jnp.arange(9 * mesh_rows, dtype=jnp.int32)[:, None]).astype(
        jnp.bfloat16
    )
    partials = jnp.dot(far_select, messages[:, 1, :], preferred_element_type=jnp.float32).reshape(
        3, 3, mesh_rows, width
    )
    from_below = shifted(partials[2], "lat", 1)
    from_above = shifted(partials[0], "lat", -1)
    row_sums = partials[1] + from_below + from_above
    from_left = passed_along(row_sums[2], "lon", 1)
    from_right = passed_along(row_sums[0], "lon", -1)
    incoming = row_sums[1] + from_left + from_right
    enc_agg = (own_part + incoming).astype(jnp.bfloat16)
    mesh_upd = jnp.dot(mesh_emb, w_mesh_self, preferred_element_type=jnp.float32) + jnp.dot(
        enc_agg, w_mesh_agg, preferred_element_type=jnp.float32
    )
    mesh_h = (mesh_emb.astype(jnp.float32) + jax.nn.silu(mesh_upd)).astype(jnp.bfloat16)
    proc_send = jnp.dot(mesh_h, w_proc_send, preferred_element_type=jnp.float32).astype(
        jnp.bfloat16
    )
    nearby = with_halo(proc_send.reshape(1, 1, mesh_rows, width), (("lat", 0), ("lon", 1)), 1)
    nearby = nearby.reshape(9 * mesh_rows, width)
    lookup = neighbour_index(mesh_src, mesh_rows, n_lon, my_lat, my_lon)
    senders = jnp.take(nearby, lookup.reshape(-1), axis=0).reshape(mesh_rows, degree, width)
    proc_recv = jnp.dot(mesh_h, w_proc_recv, preferred_element_type=jnp.float32)
    proc_msg = jax.nn.silu(
        senders.astype(jnp.float32) + proc_recv[:, None, :] + proc_dist[:, :, None] * w_proc_dist
    )
    proc_agg = jnp.sum(proc_msg, axis=1).astype(jnp.bfloat16)
    proc_upd = jnp.dot(mesh_h, w_proc_self, preferred_element_type=jnp.float32) + jnp.dot(
        proc_agg, w_proc_agg, preferred_element_type=jnp.float32
    )
    mesh_out = (mesh_h.astype(jnp.float32) + jax.nn.silu(proc_upd)).astype(jnp.bfloat16)
    dec_send = jnp.dot(mesh_out, w_dec_send, preferred_element_type=jnp.float32).astype(
        jnp.bfloat16
    )
    beside_all = with_halo(dec_send.reshape(1, 1, mesh_rows, width), (("lat", 0), ("lon", 1)), 1)
    beside_all = beside_all.reshape(9 * mesh_rows, width)
    dec_key = neighbour_index(enc_dest * mesh_rows + enc_node, mesh_rows, n_lon, my_lat, my_lon)
    fetched = jnp.take(beside_all, dec_key.reshape(-1), axis=0).reshape(cells, 2, width)
    dec_recv = jnp.dot(grid_h, w_dec_recv, preferred_element_type=jnp.float32)
    dec_msg = jax.nn.silu(
        fetched.astype(jnp.float32) + dec_recv[:, None, :] + dec_dist[:, :, None] * w_dec_dist
    )
    dec_agg = jnp.sum(dec_msg, axis=1).astype(jnp.bfloat16)
    grid_upd = jnp.dot(grid_h, w_grid_self, preferred_element_type=jnp.float32) + jnp.dot(
        dec_agg, w_grid_agg, preferred_element_type=jnp.float32
    )
    grid_z = jax.nn.silu(grid_upd).astype(jnp.bfloat16)
    pred = grid_in.astype(jnp.float32) + jnp.dot(
        grid_z, w_grid_out, preferred_element_type=jnp.float32
    )
    return pred.astype(jnp.bfloat16)


def solution(mesh):
    in_specs = (
        P(("lat", "lon"), None),
        P(("lat", "lon"), None),
        P(("lat", "lon"), None),
        P(("lat", "lon"), None),
        P(("lat", "lon"), None),
        P(("lat", "lon"), None),
        P(("lat", "lon"), None),
        P(("lat", "lon"), None),
        P(),
        P(),
        P(),
        P(),
        P(),
        P(),
        P(),
        P(),
        P(),
        P(),
        P(),
        P(),
        P(),
        P(),
        P(),
        P(),
    )
    out_specs = P(("lat", "lon"), None)
    return jax.shard_map(shards, mesh=mesh, in_specs=in_specs, out_specs=out_specs, check_vma=False)
```

profile of v0, /device:TPU:1, one launch (start us, length us, event | category | flops | bytes accessed | tf_op | source)
XLA Modules:
  0.0 290.7 jit_solution(6304662815140469666)
XLA Ops:
  0.0 0.8 fusion.53
  0.8 2.6 multiply_convert_fusion.2
  3.4 0.0 copy-start.15
  3.4 0.0 copy-start.19
  3.4 1.3 fusion.56
  4.8 2.5 multiply_convert_fusion
  7.3 2.0 copy-done.3
  9.3 10.2 %fusion = f32[4608,512]{1,0:T(8,128)S(1)} fusion(s32[2048]{0:T(1024)S(1)} %fusion.43, bf16[2048,2,512]{2,0,1:T(8,128)(2,1)S(1)} %multiply_convert_fusion), kind=kOutput, calls=%fused_computation.3 | convolution fusion | flops 9673113600 | bytes 11542528 | tf_op jit(solution)/shard_map/dot_general | solution.py:90
  19.4 2.8 fusion.52
  22.2 4.6 %collective-permute-start = (f32[3,512,512]{2,1,0:T(8,128)}, f32[3,512,512]{2,1,0:T(8,128)S(1)}, u32[]{:S(2)}, u32[]{:S(2)}) collective-permute-start(f32[3,512,512]{2,1,0:T(8,128)} %bitcast.66), channel_id=1, source_target_pairs={{0,16},{16,32},{32,48},{48,64},{64,80},{80,96},{96,112},{1,17},{17... | collective-permute-start | bytes 9437192 | tf_op jit(solution)/shard_map/ppermute | solution.py:10
  26.8 1.9 collective-permute-start.1
  28.7 32.6 %collective-permute-done = f32[3,512,512]{2,1,0:T(8,128)S(1)} collective-permute-done((f32[3,512,512]{2,1,0:T(8,128)}, f32[3,512,512]{2,1,0:T(8,128)S(1)}, u32[]{:S(2)}, u32[]{:S(2)}) %collective-permute-start) | collective-permute-done | bytes 3145760 | tf_op jit(solution)/shard_map/ppermute | solution.py:10
  61.3 4.1 %collective-permute-done.1 = f32[3,512,512]{2,1,0:T(8,128)S(1)} collective-permute-done((f32[3,512,512]{2,1,0:T(8,128)S(1)}, f32[3,512,512]{2,1,0:T(8,128)S(1)}, u32[]{:S(2)}, u32[]{:S(2)}) %collective-permute-start.1) | collective-permute-done | bytes 3145760 | tf_op jit(solution)/shard_map/ppermute | solution.py:10
  65.4 1.2 add_add_fusion
  66.5 1.7 copy-done.2
  68.2 0.2 slice_bitcast_fusion.5
  68.4 1.6 collective-permute-start.2
  69.9 4.7 %collective-permute-start.3 = (f32[512,512]{1,0:T(8,128)S(1)}, f32[512,512]{1,0:T(8,128)S(1)}, u32[]{:S(2)}, u32[]{:S(2)}) collective-permute-start(f32[512,512]{1,0:T(8,128)S(1)} %get-tuple-element.10), channel_id=1, source_target_pairs={{1,0},{2,1},{3,2},{4,3},{5,4},{6,5},{7,6},{8,7},{9,8},{10,9},{11,1... | collective-permute-start | bytes 3145736 | tf_op jit(solution)/shard_map/ppermute | solution.py:16
  74.7 1.5 fusion.55
  76.2 10.4 %collective-permute-done.2 = f32[512,512]{1,0:T(8,128)S(1)} collective-permute-done((f32[512,512]{1,0:T(8,128)S(1)}, f32[512,512]{1,0:T(8,128)S(1)}, u32[]{:S(2)}, u32[]{:S(2)}) %collective-permute-start.2) | collective-permute-done | bytes 1048608 | tf_op jit(solution)/shard_map/ppermute | solution.py:16
  86.6 1.0 copy-done.22
  87.6 0.4 copy-done.23
  88.0 4.8 %add_convert_fusion.1 = bf16[512,512]{1,0:T(8,128)(2,1)S(1)} fusion(f32[512,512]{1,0:T(8,128)} %fusion.55, bf16[512,512]{1,0:T(8,128)(2,1)} %param.38, bf16[512,512]{1,0:T(8,128)(2,1)} %param.27, f32[512,512]{1,0:T(8,128)} %copy-done.23, f32[512,512]{1,0:T(8,128)} %copy-done.22, f32[3,512,512]{2,1,0:T(8,128)} %copy-done.2, ...), kind=kOutput, calls=%fused_computation.42 | convolution fusion | flops 1346371584 | bytes 7872512 | tf_op jit(solution)/shard_map/dot_general | solution.py:100
  92.7 0.0 copy-start.18
  92.7 0.0 copy-start.17
  92.8 1.5 fusion.10
  94.2 10.8 %collective-permute-start.4 = (bf16[1,1,512,512]{3,2,1,0:T(8,128)(2,1)S(1)}, bf16[1,1,512,512]{3,2,1,0:T(8,128)(2,1)S(1)}, u32[]{:S(2)}, u32[]{:S(2)}) collective-permute-start(bf16[1,1,512,512]{3,2,1,0:T(8,128)(2,1)S(1)} %fusion.10), channel_id=1, source_target_pairs={{0,16},{16,32},{32,48},{48,64},{64,80},{80,96},{96,112},{112,0},{1... | collective-permute-start | bytes 1572872 | tf_op jit(solution)/shard_map/ppermute | solution.py:26
  105.0 6.1 %collective-permute-done.4 = bf16[1,1,512,512]{3,2,1,0:T(8,128)(2,1)S(1)} collective-permute-done((bf16[1,1,512,512]{3,2,1,0:T(8,128)(2,1)S(1)}, bf16[1,1,512,512]{3,2,1,0:T(8,128)(2,1)S(1)}, u32[]{:S(2)}, u32[]{:S(2)}) %collective-permute-start.4) | collective-permute-done | bytes 524320 | tf_op jit(solution)/shard_map/ppermute | solution.py:26
  111.2 2.9 collective-permute-done.5
  114.1 1.3 pad_maximum_fusion.2
  115.4 5.3 %collective-permute-start.7 = (bf16[3,1,512,512]{3,2,1,0:T(8,128)(2,1)}, bf16[3,1,512,512]{3,2,1,0:T(8,128)(2,1)}, u32[]{:S(2)}, u32[]{:S(2)}) collective-permute-start(bf16[3,1,512,512]{3,2,1,0:T(8,128)(2,1)} %pad_maximum_fusion.2), channel_id=1, source_target_pairs={{1,0},{2,1},{3,2},{4,3},{5,4},{6,5},{7,6},{8,7},{9,8},{10,9},{11,1... | collective-permute-start | bytes 4718600 | tf_op jit(solution)/shard_map/ppermute | solution.py:27
  120.7 0.1 fusion.26
  120.7 0.1 copy.29
  120.8 0.2 reshape.132
  121.0 0.1 copy.30
  121.1 0.0 copy-start.9
  121.2 2.5 fusion.58
  123.7 2.4 fusion.57
  126.2 22.5 %collective-permute-done.6 = bf16[3,1,512,512]{3,2,1,0:T(8,128)(2,1)} collective-permute-done((bf16[3,1,512,512]{3,2,1,0:T(8,128)(2,1)}, bf16[3,1,512,512]{3,2,1,0:T(8,128)(2,1)}, u32[]{:S(2)}, u32[]{:S(2)}) %collective-permute-start.6) | collective-permute-done | bytes 1572896 | tf_op jit(solution)/shard_map/ppermute | solution.py:26
  148.7 3.9 %pad_maximum_fusion = bf16[3,3,512,512]{3,2,1,0:T(8,128)(2,1)} fusion(bf16[3,1,512,512]{3,2,1,0:T(8,128)(2,1)} %collective-permute-done.7, bf16[1,1,512,512]{3,2,1,0:T(8,128)(2,1)S(1)} %copy-done.9, bf16[1,1,512,512]{3,2,1,0:T(8,128)(2,1)S(1)} %fusion.10, bf16[1,1,512,512]{3,2,1,0:T(8,128)(2,1)S(1)} %copy-done.5, ...), kind=kLoop, calls=%fused_computation.12 | loop fusion | flops 9437184 | bytes 9437184 | tf_op jit(solution)/shard_map/concatenate | solution.py:28
  152.6 20.4 %gather_fusion = bf16[4096,512]{1,0:T(8,128)(2,1)} fusion(bf16[4608,512]{1,0:T(8,128)(2,1)} %bitcast.62, s32[4096]{0:T(1024)S(1)} %fusion.36), kind=kCustom, calls=%fused_computation.clone | custom fusion | bytes 8404992 | tf_op jit(solution)/shard_map/jit(_take)/gather | solution.py:110
  172.9 10.0 %multiply_reduce_fusion.1 = bf16[512,512]{1,0:T(8,128)(2,1)} fusion(bf16[4096,512]{1,0:T(8,128)(2,1)} %gather_fusion, f32[512]{0:T(512)S(1)} %copy-done.20, f32[512,8]{1,0:T(8,128)S(1)} %copy.30, f32[512,512]{1,0:T(8,128)} %fusion.58, pred[4096]{0:T(1024)(128)(4,1)S(1)} %compare_and_fusion.1), kind=kLoop, calls=%fused_computation.10 | loop fusion | flops 20709376 | bytes 5789696 | tf_op jit(solution)/shard_map/reduce_sum | solution.py:115
  183.0 2.5 fusion.11
  185.5 7.7 %collective-permute-start.8 = (bf16[1,1,512,512]{3,2,1,0:T(8,128)(2,1)S(1)}, bf16[1,1,512,512]{3,2,1,0:T(8,128)(2,1)S(1)}, u32[]{:S(2)}, u32[]{:S(2)}) collective-permute-start(bf16[1,1,512,512]{3,2,1,0:T(8,128)(2,1)S(1)} %fusion.11), channel_id=1, source_target_pairs={{0,16},{16,32},{32,48},{48,64},{64,80},{80,96},{96,112},{112,0},{1... | collective-permute-start | bytes 1572872 | tf_op jit(solution)/shard_map/ppermute | solution.py:26
  193.3 6.1 %collective-permute-done.8 = bf16[1,1,512,512]{3,2,1,0:T(8,128)(2,1)S(1)} collective-permute-done((bf16[1,1,512,512]{3,2,1,0:T(8,128)(2,1)S(1)}, bf16[1,1,512,512]{3,2,1,0:T(8,128)(2,1)S(1)}, u32[]{:S(2)}, u32[]{:S(2)}) %collective-permute-start.8) | collective-permute-done | bytes 524320 | tf_op jit(solution)/shard_map/ppermute | solution.py:26
  199.4 2.9 collective-permute-done.9
  202.3 0.8 copy-done.6
  203.1 1.3 pad_maximum_fusion.3
  204.4 5.3 %collective-permute-start.11 = (bf16[3,1,512,512]{3,2,1,0:T(8,128)(2,1)}, bf16[3,1,512,512]{3,2,1,0:T(8,128)(2,1)}, u32[]{:S(2)}, u32[]{:S(2)}) collective-permute-start(bf16[3,1,512,512]{3,2,1,0:T(8,128)(2,1)} %pad_maximum_fusion.3), channel_id=1, source_target_pairs={{1,0},{2,1},{3,2},{4,3},{5,4},{6,5},{7,6},{8,7},{9,8},{10,9},{11,1... | collective-permute-start | bytes 4718600 | tf_op jit(solution)/shard_map/ppermute | solution.py:27
  209.7 0.2 fusion.31
  209.9 1.4 copy.28
  211.3 1.7 reshape.135
  213.0 0.0 copy-start.10
  213.0 4.4 %fusion.59 = f32[2048,512]{1,0:T(8,128)} fusion(bf16[2048,512]{1,0:T(8,128)(2,1)S(1)} %multiply_convert_fusion.2, bf16[512,512]{1,0:T(8,128)(2,1)} %param.45), kind=kOutput, calls=%fused_computation.133 | convolution fusion | flops 1073741824 | bytes 6815744 | tf_op jit(solution)/shard_map/dot_general | solution.py:127
  217.4 3.2 %fusion.54 = f32[2048,512]{1,0:T(8,128)} fusion(bf16[2048,512]{1,0:T(8,128)(2,1)S(1)} %multiply_convert_fusion.2, bf16[512,512]{1,0:T(8,128)(2,1)S(1)} %copy-done.10), kind=kOutput, calls=%fused_computation.128 | convolution fusion | flops 1073741824 | bytes 6815744 | tf_op jit(solution)/shard_map/dot_general | solution.py:132
  220.6 17.2 %collective-permute-done.10 = bf16[3,1,512,512]{3,2,1,0:T(8,128)(2,1)} collective-permute-done((bf16[3,1,512,512]{3,2,1,0:T(8,128)(2,1)}, bf16[3,1,512,512]{3,2,1,0:T(8,128)(2,1)}, u32[]{:S(2)}, u32[]{:S(2)}) %collective-permute-start.10) | collective-permute-done | bytes 1572896 | tf_op jit(solution)/shard_map/ppermute | solution.py:26
  237.8 3.8 %pad_maximum_fusion.1 = bf16[3,3,512,512]{3,2,1,0:T(8,128)(2,1)} fusion(bf16[3,1,512,512]{3,2,1,0:T(8,128)(2,1)} %collective-permute-done.11, bf16[1,1,512,512]{3,2,1,0:T(8,128)(2,1)S(1)} %copy-done.7, bf16[1,1,512,512]{3,2,1,0:T(8,128)(2,1)S(1)} %fusion.11, bf16[1,1,512,512]{3,2,1,0:T(8,128)(2,1)S(1)} %collective-permute-done.8, ...), kind=kLoop, calls=%fused_computation.13 | loop fusion | flops 9437184 | bytes 9437184 | tf_op jit(solution)/shard_map/concatenate | solution.py:28
  241.6 20.4 %gather_fusion.1 = bf16[4096,512]{1,0:T(8,128)(2,1)} fusion(bf16[4608,512]{1,0:T(8,128)(2,1)} %bitcast.63, s32[4096]{0:T(1024)S(1)} %fusion.37), kind=kCustom, calls=%fused_computation.1.clone | custom fusion | bytes 8404992 | tf_op jit(solution)/shard_map/jit(_take)/gather | solution.py:126
  262.0 5.2 %select_convert_fusion = f32[4096,512]{1,0:T(8,128)} fusion(bf16[4096,512]{1,0:T(8,128)(2,1)} %gather_fusion.1, pred[4096]{0:T(1024)(128)(4,1)S(1)} %compare_and_fusion), kind=kLoop, calls=%fused_computation.14 | loop fusion | flops 4194304 | bytes 12587008 | tf_op jit(solution)/shard_map/convert_element_type | solution.py:129
  267.3 10.6 %reshape.137 = f32[2048,2,512]{2,1,0:T(2,128)} reshape(f32[4096,512]{1,0:T(8,128)} %select_convert_fusion) | data formatting | bytes 16777216 | tf_op jit(solution)/shard_map/convert_element_type | solution.py:129
  277.8 0.0 copy-start.25
  277.9 6.9 %multiply_reduce_fusion = bf16[2048,512]{1,0:T(8,128)(2,1)S(1)} fusion(f32[2048,2,512]{2,1,0:T(2,128)} %reshape.137, f32[512]{0:T(512)S(1)} %copy-done.21, f32[2048,2]{0,1:T(2,128)S(1)} %copy-done.16, f32[2048,512]{1,0:T(8,128)} %fusion.59), kind=kLoop, calls=%fused_computation.9 | loop fusion | flops 15728640 | bytes 14698496 | tf_op jit(solution)/shard_map/reduce_sum | solution.py:131
  284.7 0.0 copy-start.1
  284.7 5.9 %fusion.5 = bf16[2048,227]{0,1:T(8,128)(2,1)} fusion(bf16[512,227]{0,1:T(8,128)(2,1)S(1)} %copy-done.25, bf16[2048,227]{0,1:T(8,128)(2,1)} %param.26, f32[2048,512]{1,0:T(8,128)} %fusion.54, bf16[512,512]{1,0:T(8,128)(2,1)S(1)} %copy-done.24, bf16[2048,512]{1,0:T(8,128)(2,1)S(1)} %multiply_reduce_fusion), kind=kOutput, calls=%fused_computation.21 | convolution fusion | flops 1557481472 | bytes 8907776 | tf_op jit(solution)/shard_map/dot_general | solution.py:136
  (51 shorter events, 0.2 us)
Async XLA Ops:
  0.0 3.4 %copy-start = (bf16[512,512]{1,0:T(8,128)(2,1)S(1)}, bf16[512,512]{1,0:T(8,128)(2,1)}, u32[]{:S(2)}) copy-start(bf16[512,512]{1,0:T(8,128)(2,1)} %param.35) | copy-start | bytes 1572868
  3.4 1.3 copy-start.15
  3.4 1.3 copy-start.19
  7.3 2.0 copy-start.3
  22.2 39.1 %collective-permute-start = (f32[3,512,512]{2,1,0:T(8,128)}, f32[3,512,512]{2,1,0:T(8,128)S(1)}, u32[]{:S(2)}, u32[]{:S(2)}) collective-permute-start(f32[3,512,512]{2,1,0:T(8,128)} %bitcast.66), channel_id=1, source_target_pairs={{0,16},{16,32},{32,48},{48,64},{64,80},{80,96},{96,112},{1,17},{17... | collective-permute-start | bytes 9437192 | tf_op jit(solution)/shard_map/ppermute | solution.py:10
  26.8 38.6 %collective-permute-start.1 = (f32[3,512,512]{2,1,0:T(8,128)S(1)}, f32[3,512,512]{2,1,0:T(8,128)S(1)}, u32[]{:S(2)}, u32[]{:S(2)}) collective-permute-start(f32[3,512,512]{2,1,0:T(8,128)S(1)} %bitcast.65), channel_id=1, source_target_pairs={{16,0},{32,16},{48,32},{64,48},{80,64},{96,80},{112,96},{17,1},{33... | collective-permute-start | bytes 9437192 | tf_op jit(solution)/shard_map/ppermute | solution.py:10
  66.5 1.7 copy-start.2
  68.2 6.5 %copy-start.11 = (bf16[512,512]{1,0:T(8,128)(2,1)S(1)}, bf16[512,512]{1,0:T(8,128)(2,1)}, u32[]{:S(2)}) copy-start(bf16[512,512]{1,0:T(8,128)(2,1)} %param.37) | copy-start | bytes 1572868
  68.2 6.5 %copy-start.12 = (bf16[512,512]{1,0:T(8,128)(2,1)S(1)}, bf16[512,512]{1,0:T(8,128)(2,1)}, u32[]{:S(2)}) copy-start(bf16[512,512]{1,0:T(8,128)(2,1)} %param.27) | copy-start | bytes 1572868
  68.4 18.2 %collective-permute-start.2 = (f32[512,512]{1,0:T(8,128)S(1)}, f32[512,512]{1,0:T(8,128)S(1)}, u32[]{:S(2)}, u32[]{:S(2)}) collective-permute-start(f32[512,512]{1,0:T(8,128)S(1)} %get-tuple-element.9), channel_id=1, source_target_pairs={{15,0},{0,1},{1,2},{2,3},{3,4},{4,5},{5,6},{6,7},{7,8},{8,9},{9,10... | collective-permute-start | bytes 3145736 | tf_op jit(solution)/shard_map/ppermute | solution.py:16
  69.9 16.6 %collective-permute-start.3 = (f32[512,512]{1,0:T(8,128)S(1)}, f32[512,512]{1,0:T(8,128)S(1)}, u32[]{:S(2)}, u32[]{:S(2)}) collective-permute-start(f32[512,512]{1,0:T(8,128)S(1)} %get-tuple-element.10), channel_id=1, source_target_pairs={{1,0},{2,1},{3,2},{4,3},{5,4},{6,5},{7,6},{8,7},{9,8},{10,9},{11,1... | collective-permute-start | bytes 3145736 | tf_op jit(solution)/shard_map/ppermute | solution.py:16
  86.6 1.0 copy-start.22
  86.6 1.4 copy-start.23
  92.7 27.9 %copy-start.18 = (s32[512,8]{0,1:T(8,128)S(1)}, s32[512,8]{0,1:T(8,128)}, u32[]{:S(2)}) copy-start(s32[512,8]{0,1:T(8,128)} %param.32) | copy-start | bytes 49156
  92.7 28.3 %copy-start.17 = (f32[512,8]{0,1:T(8,128)S(1)}, f32[512,8]{0,1:T(8,128)}, u32[]{:S(2)}) copy-start(f32[512,8]{0,1:T(8,128)} %param.33) | copy-start | bytes 49156
  94.2 16.9 %collective-permute-start.4 = (bf16[1,1,512,512]{3,2,1,0:T(8,128)(2,1)S(1)}, bf16[1,1,512,512]{3,2,1,0:T(8,128)(2,1)S(1)}, u32[]{:S(2)}, u32[]{:S(2)}) collective-permute-start(bf16[1,1,512,512]{3,2,1,0:T(8,128)(2,1)S(1)} %fusion.10), channel_id=1, source_target_pairs={{0,16},{16,32},{32,48},{48,64},{64,80},{80,96},{96,112},{112,0},{1... | collective-permute-start | bytes 1572872 | tf_op jit(solution)/shard_map/ppermute | solution.py:26
  105.0 9.0 %collective-permute-start.5 = (bf16[1,1,512,512]{3,2,1,0:T(8,128)(2,1)S(1)}, bf16[1,1,512,512]{3,2,1,0:T(8,128)(2,1)S(1)}, u32[]{:S(2)}, u32[]{:S(2)}) collective-permute-start(bf16[1,1,512,512]{3,2,1,0:T(8,128)(2,1)S(1)} %fusion.10), channel_id=1, source_target_pairs={{16,0},{32,16},{48,32},{64,48},{80,64},{96,80},{112,96},{0,112},{1... | collective-permute-start | bytes 1572872 | tf_op jit(solution)/shard_map/ppermute | solution.py:27
  111.2 2.9 copy-start.4
  114.0 1.4 copy-start.8
  115.4 33.3 %collective-permute-start.6 = (bf16[3,1,512,512]{3,2,1,0:T(8,128)(2,1)}, bf16[3,1,512,512]{3,2,1,0:T(8,128)(2,1)}, u32[]{:S(2)}, u32[]{:S(2)}) collective-permute-start(bf16[3,1,512,512]{3,2,1,0:T(8,128)(2,1)} %pad_maximum_fusion.2), channel_id=1, source_target_pairs={{0,1},{1,2},{2,3},{3,4},{4,5},{5,6},{6,7},{7,8},{8,9},{9,10},{10,1... | collective-permute-start | bytes 4718600 | tf_op jit(solution)/shard_map/ppermute | solution.py:26
  115.4 33.3 %collective-permute-start.7 = (bf16[3,1,512,512]{3,2,1,0:T(8,128)(2,1)}, bf16[3,1,512,512]{3,2,1,0:T(8,128)(2,1)}, u32[]{:S(2)}, u32[]{:S(2)}) collective-permute-start(bf16[3,1,512,512]{3,2,1,0:T(8,128)(2,1)} %pad_maximum_fusion.2), channel_id=1, source_target_pairs={{1,0},{2,1},{3,2},{4,3},{5,4},{6,5},{7,6},{8,7},{9,8},{10,9},{11,1... | collective-permute-start | bytes 4718600 | tf_op jit(solution)/shard_map/ppermute | solution.py:27
  121.1 27.6 %copy-start.5 = (bf16[1,1,512,512]{3,2,1,0:T(8,128)(2,1)S(1)}, bf16[1,1,512,512]{3,2,1,0:T(8,128)(2,1)}, u32[]{:S(2)}) copy-start(bf16[1,1,512,512]{3,2,1,0:T(8,128)(2,1)} %copy-done.4) | copy-start | bytes 1572868
  121.1 27.6 %copy-start.9 = (bf16[1,1,512,512]{3,2,1,0:T(8,128)(2,1)S(1)}, bf16[1,1,512,512]{3,2,1,0:T(8,128)(2,1)}, u32[]{:S(2)}) copy-start(bf16[1,1,512,512]{3,2,1,0:T(8,128)(2,1)} %copy-done.8) | copy-start | bytes 1572868
  152.6 20.4 %copy-start.20 = (f32[512]{0:T(512)S(1)}, f32[512]{0:T(512)}, u32[]{:S(2)}) copy-start(f32[512]{0:T(512)} %param.41) | copy-start | bytes 6148
  182.9 26.8 %copy-start.13 = (s32[2048,2]{0,1:T(2,128)S(1)}, s32[2048,2]{0,1:T(2,128)}, u32[]{:S(2)}) copy-start(s32[2048,2]{0,1:T(2,128)} %param.29) | copy-start | bytes 49156
  182.9 26.8 %copy-start.14 = (s32[2048,2]{0,1:T(2,128)S(1)}, s32[2048,2]{0,1:T(2,128)}, u32[]{:S(2)}) copy-start(s32[2048,2]{0,1:T(2,128)} %param.28) | copy-start | bytes 49156
  185.5 13.9 %collective-permute-start.8 = (bf16[1,1,512,512]{3,2,1,0:T(8,128)(2,1)S(1)}, bf16[1,1,512,512]{3,2,1,0:T(8,128)(2,1)S(1)}, u32[]{:S(2)}, u32[]{:S(2)}) collective-permute-start(bf16[1,1,512,512]{3,2,1,0:T(8,128)(2,1)S(1)} %fusion.11), channel_id=1, source_target_pairs={{0,16},{16,32},{32,48},{48,64},{64,80},{80,96},{96,112},{112,0},{1... | collective-permute-start | bytes 1572872 | tf_op jit(solution)/shard_map/ppermute | solution.py:26
  193.3 9.0 %collective-permute-start.9 = (bf16[1,1,512,512]{3,2,1,0:T(8,128)(2,1)S(1)}, bf16[1,1,512,512]{3,2,1,0:T(8,128)(2,1)S(1)}, u32[]{:S(2)}, u32[]{:S(2)}) collective-permute-start(bf16[1,1,512,512]{3,2,1,0:T(8,128)(2,1)S(1)} %fusion.11), channel_id=1, source_target_pairs={{16,0},{32,16},{48,32},{64,48},{80,64},{96,80},{112,96},{0,112},{1... | collective-permute-start | bytes 1572872 | tf_op jit(solution)/shard_map/ppermute | solution.py:27
  202.3 0.8 copy-start.6
  204.4 33.4 %collective-permute-start.10 = (bf16[3,1,512,512]{3,2,1,0:T(8,128)(2,1)}, bf16[3,1,512,512]{3,2,1,0:T(8,128)(2,1)}, u32[]{:S(2)}, u32[]{:S(2)}) collective-permute-start(bf16[3,1,512,512]{3,2,1,0:T(8,128)(2,1)} %pad_maximum_fusion.3), channel_id=1, source_target_pairs={{0,1},{1,2},{2,3},{3,4},{4,5},{5,6},{6,7},{7,8},{8,9},{9,10},{10,1... | collective-permute-start | bytes 4718600 | tf_op jit(solution)/shard_map/ppermute | solution.py:26
  204.4 33.4 %collective-permute-start.11 = (bf16[3,1,512,512]{3,2,1,0:T(8,128)(2,1)}, bf16[3,1,512,512]{3,2,1,0:T(8,128)(2,1)}, u32[]{:S(2)}, u32[]{:S(2)}) collective-permute-start(bf16[3,1,512,512]{3,2,1,0:T(8,128)(2,1)} %pad_maximum_fusion.3), channel_id=1, source_target_pairs={{1,0},{2,1},{3,2},{4,3},{5,4},{6,5},{7,6},{8,7},{9,8},{10,9},{11,1... | collective-permute-start | bytes 4718600 | tf_op jit(solution)/shard_map/ppermute | solution.py:27
  213.0 4.4 %copy-start.10 = (bf16[512,512]{1,0:T(8,128)(2,1)S(1)}, bf16[512,512]{1,0:T(8,128)(2,1)}, u32[]{:S(2)}) copy-start(bf16[512,512]{1,0:T(8,128)(2,1)} %param.47) | copy-start | bytes 1572868
  217.4 20.4 %copy-start.7 = (bf16[1,1,512,512]{3,2,1,0:T(8,128)(2,1)S(1)}, bf16[1,1,512,512]{3,2,1,0:T(8,128)(2,1)}, u32[]{:S(2)}) copy-start(bf16[1,1,512,512]{3,2,1,0:T(8,128)(2,1)} %copy-done.6) | copy-start | bytes 1572868
  267.3 10.6 %copy-start.16 = (f32[2048,2]{0,1:T(2,128)S(1)}, f32[2048,2]{0,1:T(2,128)}, u32[]{:S(2)}) copy-start(f32[2048,2]{0,1:T(2,128)} %param.31) | copy-start | bytes 49156
  267.3 10.6 %copy-start.21 = (f32[512]{0:T(512)S(1)}, f32[512]{0:T(512)}, u32[]{:S(2)}) copy-start(f32[512]{0:T(512)} %param.46) | copy-start | bytes 6148
  277.8 6.9 %copy-start.24 = (bf16[512,512]{1,0:T(8,128)(2,1)S(1)}, bf16[512,512]{1,0:T(8,128)(2,1)}, u32[]{:S(2)}) copy-start(bf16[512,512]{1,0:T(8,128)(2,1)} %param.48) | copy-start | bytes 1572868
  277.8 6.9 %copy-start.25 = (bf16[512,227]{0,1:T(8,128)(2,1)S(1)}, bf16[512,227]{0,1:T(8,128)(2,1)}, u32[]{:S(2)}) copy-start(bf16[512,227]{0,1:T(8,128)(2,1)} %param.49) | copy-start | bytes 697348
  284.7 6.0 %copy-start.1 = (bf16[512,512]{1,0:T(8,128)(2,1)S(1)}, bf16[512,512]{1,0:T(8,128)(2,1)}, u32[]{:S(2)}) copy-start(bf16[512,512]{1,0:T(8,128)(2,1)} %param.35) | copy-start | bytes 1572868
where the time goes:
time: 296 us; the launch traced here: 291 us
  waiting for transfers between devices  105 us (35%)
  local copies, waits for them, and re-layouts  63.6 us (21%)
  matrix products  42.8 us (14%)
  starting transfers between devices  41.9 us (14%)
  other arithmetic  37.3 us (13%)
    ppermute x4, waiting for transfers between devices, with_halo(): before = lax.ppermute(last, axis, up)  52 us
    ppermute x2, waiting for transfers between devices, shifted(): return lax.ppermute(shard, axis, pairs)  36.7 us
    gather x1, local copies, waits for them, and re-layouts, shards(): jnp.take(nearby, lookup.reshape(-1), axis=0)  20.4 us
    gather x1, local copies, waits for them, and re-layouts, shards(): jnp.take(beside_all, dec_key.reshape(-1), axis=0).reshape(cells, 2, width)  20.4 us
    ppermute x4, starting transfers between devices, with_halo(): before = lax.ppermute(last, axis, up)  18.5 us
    ppermute x4, starting transfers between devices, with_halo(): after = lax.ppermute(leading, axis, down)  10.6 us
    convert_element_type x1, local copies, waits for them, and re-layouts, shards(): fetched.astype(jnp.float32) + dec_recv[:, None, :]  10.6 us
    ppermute x2, waiting for transfers between devices, passed_along(): return lax.ppermute(block, axis, route)  10.4 us
  transfers between devices with their start and end apart: 12, of which 9 were waited for; matrix products, arithmetic and copies ran while one was open for 6% of the time, Pallas kernels for 0%

commit v1 on v0

v1 whole, which is shorter than its diff:
```python
import functools

import jax
import jax.numpy as jnp
from jax import lax
from jax.experimental import pallas as pl
from jax.experimental.pallas import tpu as pltpu
from jax.sharding import PartitionSpec as P

BF16 = jnp.bfloat16
F32 = jnp.float32
I32 = jnp.int32
QUARTERS = 4

PARTNER, CROSS, LEFT, RIGHT = range(4)

XL, XR, PL_, PR, OL, OR, XC, PC = range(8)

U_OWN, U_PART, U_CROSS = 0, 1, 3
U_SIDE = {"own": (2, 5), "part": (4, 7), "cross": (6, 8)}
UNITS = 9

ENC_SEMS = 2 * QUARTERS + 2 + 2 * QUARTERS + 2
HALO_SEMS = 8 * QUARTERS


def silu(v):
    h = 0.5 * v
    return h + h * jnp.tanh(h)


def mm(a, b):
    return jnp.dot(a, b, preferred_element_type=F32)


def one_hot(keys, base, width):
    lane = lax.broadcasted_iota(I32, keys.shape, 1)
    shifted = keys - base
    pieces = [
        jnp.where(shifted == lane + g * 128, 1.0, 0.0).astype(BF16) for g in range(width // 128)
    ]
    return jnp.concatenate(pieces, axis=1)


def kernel(
    n_lat,
    n_lon,
    weights,
    grid_t,
    emb,
    dest,
    node,
    enc_d,
    dec_d,
    src,
    proc_d,
    w_enc_dist,
    w_proc_dist,
    w_dec_dist,
    *refs,
):
    hbm = dict(zip(weights, refs[: len(weights)]))
    (
        out,
        wv_all,
        w_in,
        w_out,
        cell_keys,
        cell_rows,
        cell_cols,
        key1_lanes,
        key0_lanes,
        proc_lanes,
        proc_cols,
        grid_h,
        msg,
        sb,
        rb,
        ss,
        own_c,
        pre,
        mesh_h,
        table1,
        table2,
        acc,
        u_buf,
        w_sems,
        enc_send,
        enc_recv,
        h1_send,
        h1_recv,
        h2_send,
        h2_recv,
    ) = refs[len(weights) :]
    m, width = emb.shape
    cells = grid_t.shape[1]
    degree = src.shape[0]
    quarter = m // QUARTERS
    half = m // 2
    block = min(256, cells)
    wide = min(512, cells)

    lat = lax.axis_index("lat")
    lon = lax.axis_index("lon")
    core = lat % 2
    toward = 1 - 2 * core
    partner = (lat + toward, lon)
    cross = ((lat - toward + n_lat) % n_lat, lon)
    left = (lat, (lon - 1 + n_lon) % n_lon)
    right = (lat, (lon + 1) % n_lon)
    peers = (partner, cross, left, right)

    square = [name for name in weights if name not in ("w_grid_in", "w_grid_out")]
    w_at = {name: wv_all.at[i] for i, name in enumerate(square)}
    w_at["w_grid_in"] = w_in
    w_at["w_grid_out"] = w_out
    fetches = {
        name: pltpu.make_async_copy(hbm[name], w_at[name], w_sems.at[i])
        for i, name in enumerate(weights)
    }
    for name in weights:
        fetches[name].start()
    barrier = pltpu.get_barrier_semaphore()
    for peer in peers:
        pl.semaphore_signal(
            barrier, inc=1, device_id=peer, device_id_type=pl.DeviceIdType.MESH
        )

    def weight(name):
        return w_at[name][...]

    def remote(src_ref, dst_ref, send, recv, i, peer):
        return pltpu.make_async_remote_copy(
            src_ref=src_ref,
            dst_ref=dst_ref,
            send_sem=send.at[i],
            recv_sem=recv.at[i],
            device_id=peers[peer],
            device_id_type=pl.DeviceIdType.MESH,
        )

    shift = m.bit_length() - 1
    lon_shift = n_lon.bit_length() - 1

    def places(patch):
        d_row = (patch >> lon_shift) - lat
        side = ((patch & (n_lon - 1)) - lon + 1) & (n_lon - 1)
        return d_row == 0, d_row == toward, side

    def gather_key(patch, at):
        own, part, side = places(patch)
        upper = (at >= half).astype(I32)
        centre = jnp.where(own, U_OWN, jnp.where(part, U_PART, U_CROSS)) * m + at
        first = jnp.where(own, U_SIDE["own"][0], jnp.where(part, U_SIDE["part"][0], U_SIDE["cross"][0]))
        second = jnp.where(own, U_SIDE["own"][1], jnp.where(part, U_SIDE["part"][1], U_SIDE["cross"][1]))
        unit = jnp.where(upper == 1, second, first)
        beside = unit * m + jnp.where(side == 2, half, 0) + at - upper * half
        return jnp.where(side == 1, centre, beside)

    patch1 = dest[1:2, :]
    node1 = node[1:2, :]
    own1, part1, side1 = places(patch1)
    slot_l = jnp.where(own1, OL, jnp.where(part1, PL_, XL))
    slot_r = jnp.where(own1, OR, jnp.where(part1, PR, XR))
    slot_c = jnp.where(part1, PC, XC)
    slot = jnp.where(side1 == 0, slot_l, jnp.where(side1 == 2, slot_r, slot_c))
    cell_rows[0:1, :] = slot * m + node1
    cell_rows[1:2, :] = node[0:1, :]
    cell_keys[...] = jnp.zeros_like(cell_keys)
    cell_keys[0:1, :] = node[0:1, :].astype(F32)
    cell_keys[1:2, :] = gather_key(patch1, node1).astype(F32)
    cell_keys[2:4, :] = enc_d[...]
    cell_keys[4:6, :] = dec_d[...]
    cell_cols[...] = jnp.transpose(cell_keys[...])
    mesh_key = gather_key(src[...] >> shift, src[...] & (m - 1)).astype(F32)
    mesh_key_t = jnp.transpose(mesh_key)
    proc_cols[...] = jnp.transpose(proc_d[...])
    for j in range(degree):
        proc_lanes[j] = jnp.broadcast_to(mesh_key_t[:, j : j + 1], (m, 128)).astype(I32)

    fetches["w_grid_in"].wait()
    fetches["w_enc_src"].wait()

    def embed(b, carry):
        rows = pl.ds(pl.multiple_of(b * block, block), block)
        part = grid_t[:, rows]
        h = silu(
            lax.dot_general(part, w_in[...], (((0,), (0,)), ((), ())), preferred_element_type=F32)
        ).astype(BF16)
        grid_h[rows, :] = h
        e = mm(h, weight("w_enc_src"))
        cols = cell_cols[rows, :]
        for k in range(2):
            msg[k, rows, :] = silu(e + cols[:, 2 + k : 3 + k] * w_enc_dist[...]).astype(BF16)
        key0_lanes[rows, :] = jnp.broadcast_to(cols[:, 0:1], (block, 128)).astype(I32)
        key1_lanes[rows, :] = jnp.broadcast_to(cols[:, 1:2], (block, 128)).astype(I32)
        return carry

    lax.fori_loop(0, cells // block, embed, 0)
    pl.semaphore_wait(barrier, 4)

    def enc_x(side, q):
        rows = pl.ds(q * quarter, quarter)
        return remote(
            sb.at[side, rows], rb.at[side, rows], enc_send, enc_recv, 2 * q + side, CROSS
        )

    def enc_p(side):
        return remote(
            sb.at[2 + side], rb.at[2 + side], enc_send, enc_recv, 2 * QUARTERS + side, PARTNER
        )

    def enc_side(side, q):
        rows = pl.ds(q * quarter, quarter)
        return remote(
            ss.at[side, rows],
            rb.at[4 + side, rows],
            enc_send,
            enc_recv,
            2 * QUARTERS + 2 + 2 * q + side,
            LEFT if side == 0 else RIGHT,
        )

    def enc_c(which):
        return remote(
            sb.at[XC + which],
            rb.at[XC + which],
            enc_send,
            enc_recv,
            4 * QUARTERS + 2 + which,
            CROSS if which == 0 else PARTNER,
        )

    def relay_sums(q):
        rows = pl.ds(q * quarter, quarter)
        for side in range(2):
            enc_x(side, q).wait_recv()
            if q == 0:
                enc_p(side).wait_recv()
            total = (
                sb[4 + side, rows, :].astype(F32)
                + rb[side, rows, :].astype(F32)
                + rb[2 + side, rows, :].astype(F32)
            )
            ss[side, rows, :] = total.astype(BF16)
        for side in range(2):
            enc_side(side, q).start()

    def scatter(row, base, which):
        keys = cell_rows[row : row + 1, :] - base
        sel = jnp.where(lax.broadcasted_iota(I32, (m, cells), 0) == keys, 1.0, 0.0).astype(BF16)
        return mm(sel, msg[which])

    def partial_step(s, carry):
        sb[s] = scatter(0, s * m, 1).astype(BF16)

        @pl.when(s == XR)
        def _():
            for q in range(QUARTERS):
                for side in range(2):
                    enc_x(side, q).start()

        @pl.when(s == PR)
        def _():
            for side in range(2):
                enc_p(side).start()

        @pl.when(s == OR)
        def _():
            relay_sums(0)

        @pl.when(s == XC)
        def _():
            enc_c(0).start()
            relay_sums(1)

        @pl.when(s == PC)
        def _():
            enc_c(1).start()
            relay_sums(2)

        return carry

    lax.fori_loop(0, 8, partial_step, 0)
    own_c[...] = scatter(1, 0, 0)
    relay_sums(3)

    fetches["w_mesh_self"].wait()
    fetches["w_mesh_agg"].wait()
    fetches["w_proc_send"].wait()
    pre[...] = mm(emb[...], weight("w_mesh_self"))
    enc_c(0).wait_recv()
    enc_c(1).wait_recv()

    def halo(table, send, recv):
        def own(q, peer):
            src_ref = table.at[U_OWN, pl.ds(q * quarter, quarter)]
            if peer == PARTNER:
                dst = table.at[U_PART, pl.ds(q * quarter, quarter)]
            elif peer == CROSS:
                dst = table.at[U_CROSS, pl.ds(q * quarter, quarter)]
            else:
                dst = side_rows("own", 1 if peer == LEFT else 0, q)
            return remote(src_ref, dst, send, recv, 4 * q + peer, peer)

        def side_rows(owner, side, q):
            unit = U_SIDE[owner][q // 2]
            return table.at[unit, pl.ds(side * half + (q % 2) * quarter, quarter)]

        def forward(side, q, peer):
            dst = side_rows("part" if peer == PARTNER else "cross", side, q)
            index = 4 * QUARTERS + 4 * q + 2 * side + peer
            return remote(side_rows("own", side, q), dst, send, recv, index, peer)

        def start_own(q):
            for peer in (LEFT, RIGHT, CROSS, PARTNER):
                own(q, peer).start()

        def pass_on(q):
            own(q, RIGHT).wait_recv()
            own(q, LEFT).wait_recv()
            for side in range(2):
                forward(side, q, CROSS).start()
                forward(side, q, PARTNER).start()

        def wait_forwarded(peer, quarters):
            for q in quarters:
                for side in range(2):
                    forward(side, q, peer).wait_recv()

        def before(u):
            @pl.when(u == 1)
            def _():
                for q in range(QUARTERS):
                    own(q, PARTNER).wait_recv()

            @pl.when(u == 2)
            def _():
                pass_on(0)
                pass_on(1)

            @pl.when(u == 3)
            def _():
                for q in range(QUARTERS):
                    own(q, CROSS).wait_recv()

            @pl.when(u == 4)
            def _():
                pass_on(2)
                wait_forwarded(PARTNER, (0, 1))

            @pl.when(u == 5)
            def _():
                pass_on(3)

            @pl.when(u == 6)
            def _():
                wait_forwarded(CROSS, (0, 1))

            @pl.when(u == 7)
            def _():
                wait_forwarded(PARTNER, (2, 3))

        def before_last():
            wait_forwarded(CROSS, (2, 3))

        def finish():
            for q in range(QUARTERS):
                for peer in range(4):
                    own(q, peer).wait_send()
                for side in range(2):
                    for peer in (PARTNER, CROSS):
                        forward(side, q, peer).wait_send()

        return start_own, before, before_last, finish

    start1, before1, last1, finish1 = halo(table1, h1_send, h1_recv)
    start2, before2, last2, finish2 = halo(table2, h2_send, h2_recv)

    for q in range(QUARTERS):
        rows = pl.ds(q * quarter, quarter)
        for side in range(2):
            enc_side(side, q).wait_recv()
        total = own_c[rows, :]
        for i in range(4, 8):
            total = total + rb[i, rows, :].astype(F32)
        upd = pre[rows, :] + mm(total.astype(BF16), weight("w_mesh_agg"))
        h = (emb[rows, :].astype(F32) + silu(upd)).astype(BF16)
        mesh_h[rows, :] = h
        table1[U_OWN, rows, :] = mm(h, weight("w_proc_send")).astype(BF16)
        start1(q)

    fetches["w_proc_recv"].wait()
    fetches["w_proc_self"].wait()
    fetches["w_proc_agg"].wait()
    fetches["w_dec_send"].wait()
    pre[...] = mm(mesh_h[...], weight("w_proc_recv"))
    for j in range(degree):
        acc[pl.ds(j * m, m), :] = pre[...] + proc_cols[:, j : j + 1] * w_proc_dist[...]
    own_c[...] = mm(mesh_h[...], weight("w_proc_self"))

    def proc_rows(j):
        return pl.ds(pl.multiple_of(j * m, m), m)

    def proc_unit(u, carry):
        before1(u)

        def edge(j, c):
            rows = proc_rows(j)
            acc[rows, :] += mm(one_hot(proc_lanes[j], u * m, m), table1[u])
            return c

        lax.fori_loop(0, degree, edge, 0)
        return carry

    lax.fori_loop(0, UNITS - 1, proc_unit, 0)
    last1()
    pre[...] = jnp.zeros_like(pre)

    def last_edge(j, c):
        rows = proc_rows(j)
        full = acc[rows, :] + mm(one_hot(proc_lanes[j], (UNITS - 1) * m, m), table1[UNITS - 1])
        pre[...] += silu(full)
        return c

    lax.fori_loop(0, degree, last_edge, 0)
    for q in range(QUARTERS):
        rows = pl.ds(q * quarter, quarter)
        upd = own_c[rows, :] + mm(pre[rows, :].astype(BF16), weight("w_proc_agg"))
        h = (mesh_h[rows, :].astype(F32) + silu(upd)).astype(BF16)
        table2[U_OWN, rows, :] = mm(h, weight("w_dec_send")).astype(BF16)
        start2(q)

    for name in ("w_dec_recv", "w_grid_self", "w_grid_agg", "w_grid_out"):
        fetches[name].wait()

    def cell_block(b):
        return pl.ds(pl.multiple_of(b * wide, wide), wide)

    def second(b):
        return pl.ds(pl.multiple_of(cells + b * wide, wide), wide)

    def first_edges(b, c):
        rows = cell_block(b)
        h = grid_h[rows, :]
        recv = mm(h, weight("w_dec_recv"))
        cols = cell_cols[rows, :]
        acc[second(b), :] = recv + cols[:, 5:6] * w_dec_dist[...]
        near = recv + cols[:, 4:5] * w_dec_dist[...]
        near = near + mm(one_hot(key0_lanes[rows, :], 0, m), table2[U_OWN])
        acc[rows, :] = silu(near)
        u_buf[rows, :] = mm(h, weight("w_grid_self"))
        return c

    lax.fori_loop(0, cells // wide, first_edges, 0)

    def dec_unit(u, carry):
        before2(u)

        def edge(b, c):
            acc[second(b), :] += mm(one_hot(key1_lanes[cell_block(b), :], u * m, m), table2[u])
            return c

        lax.fori_loop(0, cells // wide, edge, 0)
        return carry

    lax.fori_loop(1, UNITS - 1, dec_unit, 0)
    last2()

    def finish_cells(b, c):
        rows = cell_block(b)
        far = acc[second(b), :] + mm(
            one_hot(key1_lanes[rows, :], (UNITS - 1) * m, m), table2[UNITS - 1]
        )
        agg = (acc[rows, :] + silu(far)).astype(BF16)
        z = silu(u_buf[rows, :] + mm(agg, weight("w_grid_agg"))).astype(BF16)
        change = lax.dot_general(
            w_out[...], z, (((1,), (1,)), ((), ())), preferred_element_type=F32
        )
        out[:, rows] = (grid_t[:, rows].astype(F32) + change).astype(BF16)
        return c

    lax.fori_loop(0, cells // wide, finish_cells, 0)

    for side in range(2):
        for q in range(QUARTERS):
            enc_x(side, q).wait_send()
            enc_side(side, q).wait_send()
        enc_p(side).wait_send()
        enc_c(side).wait_send()
    finish1()
    finish2()


SQUARE = (
    "w_enc_src",
    "w_mesh_self",
    "w_mesh_agg",
    "w_proc_send",
    "w_proc_recv",
    "w_proc_self",
    "w_proc_agg",
    "w_dec_send",
    "w_dec_recv",
    "w_grid_self",
    "w_grid_agg",
)
WEIGHTS = ("w_grid_in",) + SQUARE + ("w_grid_out",)


def shards(
    grid_in,
    mesh_emb,
    enc_dest,
    enc_node,
    enc_dist,
    dec_dist,
    mesh_src,
    proc_dist,
    w_grid_in,
    w_enc_src,
    w_enc_dist,
    w_mesh_self,
    w_mesh_agg,
    w_proc_send,
    w_proc_recv,
    w_proc_dist,
    w_proc_self,
    w_proc_agg,
    w_dec_send,
    w_dec_recv,
    w_dec_dist,
    w_grid_self,
    w_grid_agg,
    w_grid_out,
):
    n_lat, n_lon = lax.axis_size("lat"), lax.axis_size("lon")
    cells, variables = grid_in.shape
    m, width = mesh_emb.shape
    degree = mesh_src.shape[1]
    local = locals()
    hbm = [local[name] for name in WEIGHTS[:-1]] + [w_grid_out.T]
    vmem = pl.BlockSpec(memory_space=pltpu.VMEM)
    any_space = pl.BlockSpec(memory_space=pl.ANY)
    rows = max(degree * m, 2 * cells)
    out = pl.pallas_call(
        functools.partial(kernel, n_lat, n_lon, WEIGHTS),
        out_shape=jax.ShapeDtypeStruct((variables, cells), BF16),
        in_specs=[vmem] * 11 + [any_space] * len(WEIGHTS),
        out_specs=vmem,
        scratch_shapes=[
            pltpu.VMEM((len(SQUARE), width, width), BF16),
            pltpu.VMEM((variables, width), BF16),
            pltpu.VMEM((variables, width), BF16),
            pltpu.VMEM((8, cells), F32),
            pltpu.VMEM((8, cells), I32),
            pltpu.VMEM((cells, 8), F32),
            pltpu.VMEM((cells, 128), I32),
            pltpu.VMEM((cells, 128), I32),
            pltpu.VMEM((degree, m, 128), I32),
            pltpu.VMEM((m, degree), F32),
            pltpu.VMEM((cells, width), BF16),
            pltpu.VMEM((2, cells, width), BF16),
            pltpu.VMEM((8, m, width), BF16),
            pltpu.VMEM((8, m, width), BF16),
            pltpu.VMEM((2, m, width), BF16),
            pltpu.VMEM((m, width), F32),
            pltpu.VMEM((m, width), F32),
            pltpu.VMEM((m, width), BF16),
            pltpu.VMEM((UNITS, m, width), BF16),
            pltpu.VMEM((UNITS, m, width), BF16),
            pltpu.VMEM((rows, width), F32),
            pltpu.VMEM((cells, width), F32),
            pltpu.SemaphoreType.DMA((len(WEIGHTS),)),
            pltpu.SemaphoreType.DMA((ENC_SEMS,)),
            pltpu.SemaphoreType.DMA((ENC_SEMS,)),
            pltpu.SemaphoreType.DMA((HALO_SEMS,)),
            pltpu.SemaphoreType.DMA((HALO_SEMS,)),
            pltpu.SemaphoreType.DMA((HALO_SEMS,)),
            pltpu.SemaphoreType.DMA((HALO_SEMS,)),
        ],
        compiler_params=pltpu.CompilerParams(
            collective_id=0, has_side_effects=True, vmem_limit_bytes=67_000_000
        ),
    )(
        grid_in.T,
        mesh_emb,
        enc_dest.T,
        enc_node.T,
        enc_dist.T,
        dec_dist.T,
        mesh_src.T,
        proc_dist.T,
        w_enc_dist.reshape(1, width),
        w_proc_dist.reshape(1, width),
        w_dec_dist.reshape(1, width),
        *hbm,
    )
    return out.T


def solution(mesh):
    split = P(("lat", "lon"), None)
    in_specs = (split,) * 8 + (P(),) * 16
    return jax.shard_map(shards, mesh=mesh, in_specs=in_specs, out_specs=split, check_vma=False)
```

time: 296 us -> 104 us (0.35); the launches traced: 291 us -> 104 us
  waiting for transfers between devices: 105 us -> 0 us
  Pallas kernels: 0 us -> 102 us
  local copies, waits for them, and re-layouts: 63.6 us -> 2.22 us
  matrix products: 42.8 us -> 0 us
  starting transfers between devices: 41.9 us -> 0 us
  other arithmetic: 37.3 us -> 0 us
    ppermute x12 -> x0, waiting for transfers between devices: 105 us -> none  [the longest x4 52 us: with_halo(): before = lax.ppermute(last, axis, up)]
    pallas_call x0 -> x1, Pallas kernels: none -> 102 us  [shards(): pl.pallas_call(functools.partial(kernel, n_lat, n_lon, WEIGHTS), out_shap...]
    dot_general x12 -> x0, matrix products: 42.8 us -> none  [the longest x1 10.2 us: shards(): jnp.dot(far_select, messages[:, 1, :], preferred_element_type=jnp.float32)]
    ppermute x12 -> x0, starting transfers between devices: 41.9 us -> none  [the longest x4 18.5 us: with_halo(): before = lax.ppermute(last, axis, up)]
    gather x2 -> x0, local copies, waits for them, and re-layouts: 40.7 us -> none  [the longest x1 20.4 us: shards(): jnp.take(nearby, lookup.reshape(-1), axis=0)]
    reduce_sum x2 -> x0, other arithmetic: 16.9 us -> none  [the longest x1 10 us: shards(): proc_agg = jnp.sum(proc_msg, axis=1).astype(jnp.bfloat16)]
    convert_element_type x1 -> x0, local copies, waits for them, and re-layouts: 10.6 us -> none  [shards(): fetched.astype(jnp.float32) + dec_recv[:, None, :]]
    concatenate x4 -> x0, other arithmetic: 10.4 us -> none  [with_halo(): shard = jnp.concatenate([before, shard, after], axis=dim)]
  transfers between devices with their start and end apart: 12 -> 0, of which waited for: 9 -> 0; matrix products, arithmetic and copies ran while one was open for 6% -> 0% of each run, Pallas kernels for 0% -> 0%
where the time goes in v1:
time: 104 us
  Pallas kernels  102 us (98%)
  local copies, waits for them, and re-layouts  2.22 us (2%)
    pallas_call x1, Pallas kernels, shards(): pl.pallas_call(functools.partial(kernel, n_lat, n_lon, WEIGHTS), out_shap...  102 us
    unnamed x1, local copies, waits for them, and re-layouts  2.22 us

profile of v1, /device:TPU:1, one launch (start us, length us, event | category | flops | bytes accessed | tf_op | source)
XLA Modules:
  0.0 103.7 jit_solution(10555469631090696108)
XLA Ops:
  0.0 101.5 %shard_map.226 = bf16[227,2048]{1,0:T(8,128)(2,1)} custom-call(bf16[227,2048]{1,0:T(8,128)(2,1)} %bitcast.13, bf16[512,512]{1,0:T(8,128)(2,1)} %emb.1, s32[2,2048]{1,0:T(2,128)} %bitcast.15, s32[2,2048]{1,0:T(2,128)} %bitcast.16, f32[2,2048]{1,0:T(2,128)} %bitcast.17, f32[2,2048]{1,0:T(2,128)} %bitcast.18, s32[8,512]{1,0:T(8,128)} %bitcast.19, ...), custom_call_target="tpu_custom_call" | custom-call | tf_op jit(solution)/shard_map/pallas_call | solution.py:546
  101.5 2.2 %copy.26 = bf16[2048,227]{0,1:T(8,128)(2,1)} copy(bf16[2048,227]{0,1:T(8,128)(2,1)} %bitcast.12) | data formatting | bytes 1859584

commit v2 on v1

--- a/solution.py
+++ b/solution.py
@@ -11,6 +11,8 @@
 F32 = jnp.float32
 I32 = jnp.int32
 QUARTERS = 4
+LAST = QUARTERS - 1
+ORDER = (LAST,) + tuple(range(LAST))
 
 PARTNER, CROSS, LEFT, RIGHT = range(4)
 
@@ -24,9 +26,12 @@
 HALO_SEMS = 8 * QUARTERS
 
 
+def silu_of_half(h):
+    return h + h * jnp.tanh(h)
+
+
 def silu(v):
-    h = 0.5 * v
-    return h + h * jnp.tanh(h)
+    return silu_of_half(0.5 * v)
 
 
 def mm(a, b):
@@ -83,6 +88,8 @@
         table1,
         table2,
         acc,
+        near_buf,
+        far_buf,
         u_buf,
         w_sems,
         enc_send,
@@ -176,7 +183,11 @@
     mesh_key_t = jnp.transpose(mesh_key)
     proc_cols[...] = jnp.transpose(proc_d[...])
     for j in range(degree):
-        proc_lanes[j] = jnp.broadcast_to(mesh_key_t[:, j : j + 1], (m, 128)).astype(I32)
+        lanes = jnp.broadcast_to(mesh_key_t[:, j : j + 1], (m, 128)).astype(I32)
+        for q in range(QUARTERS):
+            proc_lanes[pl.ds((q * degree + j) * quarter, quarter), :] = lanes[
+                q * quarter : (q + 1) * quarter
+            ]
 
     fetches["w_grid_in"].wait()
     fetches["w_enc_src"].wait()
@@ -188,10 +199,11 @@
             lax.dot_general(part, w_in[...], (((0,), (0,)), ((), ())), preferred_element_type=F32)
         ).astype(BF16)
         grid_h[rows, :] = h
-        e = mm(h, weight("w_enc_src"))
+        e = 0.5 * mm(h, weight("w_enc_src"))
         cols = cell_cols[rows, :]
+        half_dist = 0.5 * w_enc_dist[...]
         for k in range(2):
-            msg[k, rows, :] = silu(e + cols[:, 2 + k : 3 + k] * w_enc_dist[...]).astype(BF16)
+            msg[k, rows, :] = silu_of_half(e + cols[:, 2 + k : 3 + k] * half_dist).astype(BF16)
         key0_lanes[rows, :] = jnp.broadcast_to(cols[:, 0:1], (block, 128)).astype(I32)
         key1_lanes[rows, :] = jnp.broadcast_to(cols[:, 1:2], (block, 128)).astype(I32)
         return carry
@@ -246,19 +258,34 @@
         for side in range(2):
             enc_side(side, q).start()
 
-    def scatter(row, base, which):
+    def scatter(row, base, which, rows):
         keys = cell_rows[row : row + 1, :] - base
-        sel = jnp.where(lax.broadcasted_iota(I32, (m, cells), 0) == keys, 1.0, 0.0).astype(BF16)
+        sel = jnp.where(lax.broadcasted_iota(I32, (rows, cells), 0) == keys, 1.0, 0.0).astype(BF16)
         return mm(sel, msg[which])
 
+    def cell_block(b):
+        return pl.ds(b * wide, wide)
+
+    def cell_terms(blocks):
+        for b in blocks:
+            rows = cell_block(b)
+            h = grid_h[rows, :]
+            recv = mm(h, weight("w_dec_recv"))
+            cols = cell_cols[rows, :]
+            near_buf[rows, :] = recv + cols[:, 4:5] * w_dec_dist[...]
+            far_buf[rows, :] = recv + cols[:, 5:6] * w_dec_dist[...]
+            u_buf[rows, :] = mm(h, weight("w_grid_self"))
+
+    for upper in range(2):
+        for side in range(2):
+            part = scatter(0, side * m + upper * half, 1, half)
+            sb[side, pl.ds(upper * half, half), :] = part.astype(BF16)
+        for q in range(2 * upper, 2 * upper + 2):
+            for side in range(2):
+                enc_x(side, q).start()
+
     def partial_step(s, carry):
-        sb[s] = scatter(0, s * m, 1).astype(BF16)
-
-        @pl.when(s == XR)
-        def _():
-            for q in range(QUARTERS):
-                for side in range(2):
-                    enc_x(side, q).start()
+        sb[s] = scatter(0, s * m, 1, m).astype(BF16)
 
         @pl.when(s == PR)
         def _():
@@ -272,17 +299,22 @@
         @pl.when(s == XC)
         def _():
             enc_c(0).start()
-            relay_sums(1)
 
         @pl.when(s == PC)
         def _():
             enc_c(1).start()
-            relay_sums(2)
 
         return carry
 
-    lax.fori_loop(0, 8, partial_step, 0)
-    own_c[...] = scatter(1, 0, 0)
+    lax.fori_loop(2, 8, partial_step, 0)
+    relay_sums(1)
+    own_c[...] = scatter(1, 0, 0, m)
+    fetches["w_dec_recv"].wait()
+    fetches["w_grid_self"].wait()
+    blocks = cells // wide
+    cell_terms(range(0, blocks // 2))
+    relay_sums(2)
+    cell_terms(range(blocks // 2, blocks))
     relay_sums(3)
 
     fetches["w_mesh_self"].wait()
@@ -310,6 +342,9 @@
         def forward(side, q, peer):
             dst = side_rows("part" if peer == PARTNER else "cross", side, q)
             index = 4 * QUARTERS + 4 * q + 2 * side + peer
+            if peer == CROSS and q == LAST:
+                src_ref = table.at[U_CROSS, pl.ds(q * quarter, quarter)]
+                return remote(src_ref, dst, send, recv, index, RIGHT if side == 0 else LEFT)
             return remote(side_rows("own", side, q), dst, send, recv, index, peer)
 
         def start_own(q):
@@ -320,8 +355,14 @@
             own(q, RIGHT).wait_recv()
             own(q, LEFT).wait_recv()
             for side in range(2):
-                forward(side, q, CROSS).start()
+                if q != LAST:
+                    forward(side, q, CROSS).start()
                 forward(side, q, PARTNER).start()
+
+        def turn_corner():
+            own(LAST, CROSS).wait_recv()
+            for side in range(2):
+                forward(side, LAST, CROSS).start()
 
         def wait_forwarded(peer, quarters):
             for q in quarters:
@@ -329,20 +370,15 @@
                     forward(side, q, peer).wait_recv()
 
         def before(u):
-            @pl.when(u == 1)
-            def _():
-                for q in range(QUARTERS):
-                    own(q, PARTNER).wait_recv()
-
             @pl.when(u == 2)
             def _():
-                pass_on(0)
                 pass_on(1)
 
             @pl.when(u == 3)
             def _():
                 for q in range(QUARTERS):
-                    own(q, CROSS).wait_recv()
+                    if q != LAST:
+                        own(q, CROSS).wait_recv()
 
             @pl.when(u == 4)
             def _():
@@ -351,17 +387,20 @@
 
             @pl.when(u == 5)
             def _():
-                pass_on(3)
+                pass_on(LAST)
 
             @pl.when(u == 6)
             def _():
                 wait_forwarded(CROSS, (0, 1))
 
-            @pl.when(u == 7)
-            def _():
-                wait_forwarded(PARTNER, (2, 3))
-
-        def before_last():
+        def before_partner():
+            for q in range(QUARTERS):
+                own(q, PARTNER).wait_recv()
+
+        def before_last(units):
+            if 6 in units:
+                wait_forwarded(CROSS, (0, 1))
+            wait_forwarded(PARTNER, (2, 3))
             wait_forwarded(CROSS, (2, 3))
 
         def finish():
@@ -372,12 +411,12 @@
                     for peer in (PARTNER, CROSS):
                         forward(side, q, peer).wait_send()
 
-        return start_own, before, before_last, finish
-
-    start1, before1, last1, finish1 = halo(table1, h1_send, h1_recv)
-    start2, before2, last2, finish2 = halo(table2, h2_send, h2_recv)
-
-    for q in range(QUARTERS):
+        return start_own, before_partner, pass_on, turn_corner, before, before_last, finish
+
+    start1, partner1, pass1, turn1, before1, last1, finish1 = halo(table1, h1_send, h1_recv)
+    start2, partner2, pass2, turn2, before2, last2, finish2 = halo(table2, h2_send, h2_recv)
+
+    for q in ORDER:
         rows = pl.ds(q * quarter, quarter)
         for side in range(2):
             enc_side(side, q).wait_recv()
@@ -390,97 +429,91 @@
         table1[U_OWN, rows, :] = mm(h, weight("w_proc_send")).astype(BF16)
         start1(q)
 
-    fetches["w_proc_recv"].wait()
-    fetches["w_proc_self"].wait()
-    fetches["w_proc_agg"].wait()
-    fetches["w_dec_send"].wait()
+    for name in ("w_proc_recv", "w_proc_self", "w_proc_agg", "w_dec_send"):
+        fetches[name].wait()
     pre[...] = mm(mesh_h[...], weight("w_proc_recv"))
-    for j in range(degree):
-        acc[pl.ds(j * m, m), :] = pre[...] + proc_cols[:, j : j + 1] * w_proc_dist[...]
     own_c[...] = mm(mesh_h[...], weight("w_proc_self"))
-
-    def proc_rows(j):
-        return pl.ds(pl.multiple_of(j * m, m), m)
+    group = 2 * QUARTERS
+    edge_rows = degree * m // group
+    per_group = edge_rows // quarter
+
+    def edges(g):
+        return pl.ds(g * edge_rows, edge_rows)
+
+    def units(table, first, last):
+        return table[first:last].reshape((last - first) * m, width)
+
+    partner1()
+    for g in range(group):
+        parts = []
+        for e in range(g * per_group, (g + 1) * per_group):
+            rows = pl.ds(e // degree * quarter, quarter)
+            j = e % degree
+            parts.append(pre[rows, :] + proc_cols[rows, j : j + 1] * w_proc_dist[...])
+        base = jnp.concatenate(parts, axis=0)
+        acc[edges(g), :] = base + mm(
+            one_hot(proc_lanes[edges(g), :], 0, 2 * m), units(table1, 0, 2)
+        )
+    pass1(0)
+    turn1()
 
     def proc_unit(u, carry):
         before1(u)
-
-        def edge(j, c):
-            rows = proc_rows(j)
-            acc[rows, :] += mm(one_hot(proc_lanes[j], u * m, m), table1[u])
-            return c
-
-        lax.fori_loop(0, degree, edge, 0)
+        for g in range(group):
+            acc[edges(g), :] += mm(one_hot(proc_lanes[edges(g), :], u * m, m), table1[u])
         return carry
 
-    lax.fori_loop(0, UNITS - 1, proc_unit, 0)
-    last1()
-    pre[...] = jnp.zeros_like(pre)
-
-    def last_edge(j, c):
-        rows = proc_rows(j)
-        full = acc[rows, :] + mm(one_hot(proc_lanes[j], (UNITS - 1) * m, m), table1[UNITS - 1])
-        pre[...] += silu(full)
-        return c
-
-    lax.fori_loop(0, degree, last_edge, 0)
-    for q in range(QUARTERS):
+    lax.fori_loop(2, 6, proc_unit, 0)
+    last1((6, 7, 8))
+    for q in ORDER:
         rows = pl.ds(q * quarter, quarter)
-        upd = own_c[rows, :] + mm(pre[rows, :].astype(BF16), weight("w_proc_agg"))
+        agg = None
+        for g in range(q * degree // per_group, (q + 1) * degree // per_group):
+            full = acc[edges(g), :] + mm(
+                one_hot(proc_lanes[edges(g), :], 6 * m, 3 * m), units(table1, 6, 9)
+            )
+            messages = silu(full)
+            for i in range(per_group):
+                one = messages[i * quarter : (i + 1) * quarter]
+                agg = one if agg is None else agg + one
+        upd = own_c[rows, :] + mm(agg.astype(BF16), weight("w_proc_agg"))
         h = (mesh_h[rows, :].astype(F32) + silu(upd)).astype(BF16)
         table2[U_OWN, rows, :] = mm(h, weight("w_dec_send")).astype(BF16)
         start2(q)
 
-    for name in ("w_dec_recv", "w_grid_self", "w_grid_agg", "w_grid_out"):
-        fetches[name].wait()
-
-    def cell_block(b):
-        return pl.ds(pl.multiple_of(b * wide, wide), wide)
-
-    def second(b):
-        return pl.ds(pl.multiple_of(cells + b * wide, wide), wide)
-
-    def first_edges(b, c):
+    for b in range(cells // wide):
         rows = cell_block(b)
-        h = grid_h[rows, :]
-        recv = mm(h, weight("w_dec_recv"))
-        cols = cell_cols[rows, :]
-        acc[second(b), :] = recv + cols[:, 5:6] * w_dec_dist[...]
-        near = recv + cols[:, 4:5] * w_dec_dist[...]
-        near = near + mm(one_hot(key0_lanes[rows, :], 0, m), table2[U_OWN])
-        acc[rows, :] = silu(near)
-        u_buf[rows, :] = mm(h, weight("w_grid_self"))
-        return c
-
-    lax.fori_loop(0, cells // wide, first_edges, 0)
+        near = near_buf[rows, :] + mm(one_hot(key0_lanes[rows, :], 0, m), table2[U_OWN])
+        near_buf[rows, :] = silu(near)
+    partner2()
+    pass2(0)
+    turn2()
+    for b in range(cells // wide):
+        rows = cell_block(b)
+        far_buf[rows, :] += mm(one_hot(key1_lanes[rows, :], m, m), table2[U_PART])
 
     def dec_unit(u, carry):
         before2(u)
-
-        def edge(b, c):
-            acc[second(b), :] += mm(one_hot(key1_lanes[cell_block(b), :], u * m, m), table2[u])
-            return c
-
-        lax.fori_loop(0, cells // wide, edge, 0)
+        for b in range(cells // wide):
+            rows = cell_block(b)
+            far_buf[rows, :] += mm(one_hot(key1_lanes[rows, :], u * m, m), table2[u])
         return carry
 
-    lax.fori_loop(1, UNITS - 1, dec_unit, 0)
-    last2()
-
-    def finish_cells(b, c):
+    lax.fori_loop(2, 7, dec_unit, 0)
+    last2((7, 8))
+    fetches["w_grid_agg"].wait()
+    fetches["w_grid_out"].wait()
+    for b in range(cells // wide):
         rows = cell_block(b)
-        far = acc[second(b), :] + mm(
-            one_hot(key1_lanes[rows, :], (UNITS - 1) * m, m), table2[UNITS - 1]
-        )
-        agg = (acc[rows, :] + silu(far)).astype(BF16)
+        far = far_buf[rows, :] + mm(
+            one_hot(key1_lanes[rows, :], 7 * m, 2 * m), units(table2, 7, 9)
+        )
+        agg = (near_buf[rows, :] + silu(far)).astype(BF16)
         z = silu(u_buf[rows, :] + mm(agg, weight("w_grid_agg"))).astype(BF16)
         change = lax.dot_general(
             w_out[...], z, (((1,), (1,)), ((), ())), preferred_element_type=F32
         )
         out[:, rows] = (grid_t[:, rows].astype(F32) + change).astype(BF16)
-        return c
-
-    lax.fori_loop(0, cells // wide, finish_cells, 0)
 
     for side in range(2):
         for q in range(QUARTERS):
@@ -542,7 +575,6 @@
     hbm = [local[name] for name in WEIGHTS[:-1]] + [w_grid_out.T]
     vmem = pl.BlockSpec(memory_space=pltpu.VMEM)
     any_space = pl.BlockSpec(memory_space=pl.ANY)
-    rows = max(degree * m, 2 * cells)
     out = pl.pallas_call(
         functools.partial(kernel, n_lat, n_lon, WEIGHTS),
         out_shape=jax.ShapeDtypeStruct((variables, cells), BF16),
@@ -557,7 +589,7 @@
             pltpu.VMEM((cells, 8), F32),
             pltpu.VMEM((cells, 128), I32),
             pltpu.VMEM((cells, 128), I32),
-            pltpu.VMEM((degree, m, 128), I32),
+            pltpu.VMEM((degree * m, 128), I32),
             pltpu.VMEM((m, degree), F32),
             pltpu.VMEM((cells, width), BF16),
             pltpu.VMEM((2, cells, width), BF16),
@@ -569,7 +601,9 @@
             pltpu.VMEM((m, width), BF16),
             pltpu.VMEM((UNITS, m, width), BF16),
             pltpu.VMEM((UNITS, m, width), BF16),
-            pltpu.VMEM((rows, width), F32),
+            pltpu.VMEM((degree * m, width), F32),
+            pltpu.VMEM((cells, width), F32),
+            pltpu.VMEM((cells, width), F32),
             pltpu.VMEM((cells, width), F32),
             pltpu.SemaphoreType.DMA((len(WEIGHTS),)),
             pltpu.SemaphoreType.DMA((ENC_SEMS,)),

time: 104 us -> 91.1 us (0.88)
  Pallas kernels: 102 us -> 88.7 us
    pallas_call x1, Pallas kernels: 102 us -> 88.7 us  [shards(): pl.pallas_call(functools.partial(kernel, n_lat, n_lon, WEIGHTS), out_shap...]
where the time goes in v2:
time: 91.1 us; the launch traced here: 90.9 us
  Pallas kernels  88.7 us (97%)
  local copies, waits for them, and re-layouts  2.22 us (2%)
    pallas_call x1, Pallas kernels, shards(): pl.pallas_call(functools.partial(kernel, n_lat, n_lon, WEIGHTS), out_shap...  88.7 us
    unnamed x1, local copies, waits for them, and re-layouts  2.22 us

profile of v2, /device:TPU:1, one launch (start us, length us, event | category | flops | bytes accessed | tf_op | source)
XLA Modules:
  0.0 90.9 jit_solution(12240014716342677131)
XLA Ops:
  0.0 88.7 %shard_map.226 = bf16[227,2048]{1,0:T(8,128)(2,1)} custom-call(bf16[227,2048]{1,0:T(8,128)(2,1)} %bitcast.13, bf16[512,512]{1,0:T(8,128)(2,1)} %emb.1, s32[2,2048]{1,0:T(2,128)} %bitcast.15, s32[2,2048]{1,0:T(2,128)} %bitcast.16, f32[2,2048]{1,0:T(2,128)} %bitcast.17, f32[2,2048]{1,0:T(2,128)} %bitcast.18, s32[8,512]{1,0:T(8,128)} %bitcast.19, ...), custom_call_target="tpu_custom_call" | custom-call | tf_op jit(solution)/shard_map/pallas_call | solution.py:578
  88.7 2.2 %copy.26 = bf16[2048,227]{0,1:T(8,128)(2,1)} copy(bf16[2048,227]{0,1:T(8,128)(2,1)} %bitcast.12) | data formatting | bytes 1859584

commit v3 on v2

--- a/solution.py
+++ b/solution.py
@@ -12,7 +12,6 @@
 I32 = jnp.int32
 QUARTERS = 4
 LAST = QUARTERS - 1
-ORDER = (LAST,) + tuple(range(LAST))
 
 PARTNER, CROSS, LEFT, RIGHT = range(4)
 
@@ -22,7 +21,7 @@
 U_SIDE = {"own": (2, 5), "part": (4, 7), "cross": (6, 8)}
 UNITS = 9
 
-ENC_SEMS = 2 * QUARTERS + 2 + 2 * QUARTERS + 2
+ENC_SEMS = 5 * QUARTERS + 3
 HALO_SEMS = 8 * QUARTERS
 
 
@@ -52,7 +51,6 @@
     n_lon,
     weights,
     grid_t,
-    emb,
     dest,
     node,
     enc_d,
@@ -67,6 +65,7 @@
     hbm = dict(zip(weights, refs[: len(weights)]))
     (
         out,
+        emb,
         wv_all,
         w_in,
         w_out,
@@ -117,9 +116,10 @@
     right = (lat, (lon + 1) % n_lon)
     peers = (partner, cross, left, right)
 
-    square = [name for name in weights if name not in ("w_grid_in", "w_grid_out")]
+    square = [name for name in weights if name in SQUARE]
     w_at = {name: wv_all.at[i] for i, name in enumerate(square)}
     w_at["w_grid_in"] = w_in
+    w_at["mesh_emb"] = emb
     w_at["w_grid_out"] = w_out
     fetches = {
         name: pltpu.make_async_copy(hbm[name], w_at[name], w_sems.at[i])
@@ -191,17 +191,19 @@
 
     fetches["w_grid_in"].wait()
     fetches["w_enc_src"].wait()
+    w_in[...] = w_in[...] * 0.5
+    w_at["w_enc_src"][...] = weight("w_enc_src") * 0.5
+    half_dist = 0.5 * w_enc_dist[...]
 
     def embed(b, carry):
         rows = pl.ds(pl.multiple_of(b * block, block), block)
         part = grid_t[:, rows]
-        h = silu(
+        h = silu_of_half(
             lax.dot_general(part, w_in[...], (((0,), (0,)), ((), ())), preferred_element_type=F32)
         ).astype(BF16)
         grid_h[rows, :] = h
-        e = 0.5 * mm(h, weight("w_enc_src"))
+        e = mm(h, weight("w_enc_src"))
         cols = cell_cols[rows, :]
-        half_dist = 0.5 * w_enc_dist[...]
         for k in range(2):
             msg[k, rows, :] = silu_of_half(e + cols[:, 2 + k : 3 + k] * half_dist).astype(BF16)
         key0_lanes[rows, :] = jnp.broadcast_to(cols[:, 0:1], (block, 128)).astype(I32)
@@ -233,15 +235,14 @@
             LEFT if side == 0 else RIGHT,
         )
 
-    def enc_c(which):
+    def enc_cx(q):
+        rows = pl.ds(q * quarter, quarter)
         return remote(
-            sb.at[XC + which],
-            rb.at[XC + which],
-            enc_send,
-            enc_recv,
-            4 * QUARTERS + 2 + which,
-            CROSS if which == 0 else PARTNER,
-        )
+            sb.at[XC, rows], rb.at[XC, rows], enc_send, enc_recv, 4 * QUARTERS + 2 + q, CROSS
+        )
+
+    def enc_cp():
+        return remote(sb.at[PC], rb.at[PC], enc_send, enc_recv, 5 * QUARTERS + 2, PARTNER)
 
     def relay_sums(q):
         rows = pl.ds(q * quarter, quarter)
@@ -298,11 +299,12 @@
 
         @pl.when(s == XC)
         def _():
-            enc_c(0).start()
+            for q in range(QUARTERS):
+                enc_cx(q).start()
 
         @pl.when(s == PC)
         def _():
-            enc_c(1).start()
+            enc_cp().start()
 
         return carry
 
@@ -315,14 +317,12 @@
     cell_terms(range(0, blocks // 2))
     relay_sums(2)
     cell_terms(range(blocks // 2, blocks))
+    for name in ("mesh_emb", "w_mesh_self", "w_mesh_agg", "w_proc_send"):
+        fetches[name].wait()
+    pre[...] = mm(emb[...], weight("w_mesh_self"))
     relay_sums(3)
 
-    fetches["w_mesh_self"].wait()
-    fetches["w_mesh_agg"].wait()
-    fetches["w_proc_send"].wait()
-    pre[...] = mm(emb[...], weight("w_mesh_self"))
-    enc_c(0).wait_recv()
-    enc_c(1).wait_recv()
+    enc_cp().wait_recv()
 
     def halo(table, send, recv):
         def own(q, peer):
@@ -370,19 +370,15 @@
                     forward(side, q, peer).wait_recv()
 
         def before(u):
-            @pl.when(u == 2)
-            def _():
-                pass_on(1)
-
             @pl.when(u == 3)
             def _():
+                pass_on(2)
                 for q in range(QUARTERS):
                     if q != LAST:
                         own(q, CROSS).wait_recv()
 
             @pl.when(u == 4)
             def _():
-                pass_on(2)
                 wait_forwarded(PARTNER, (0, 1))
 
             @pl.when(u == 5)
@@ -416,10 +412,11 @@
     start1, partner1, pass1, turn1, before1, last1, finish1 = halo(table1, h1_send, h1_recv)
     start2, partner2, pass2, turn2, before2, last2, finish2 = halo(table2, h2_send, h2_recv)
 
-    for q in ORDER:
+    for q in range(QUARTERS):
         rows = pl.ds(q * quarter, quarter)
         for side in range(2):
             enc_side(side, q).wait_recv()
+        enc_cx(q).wait_recv()
         total = own_c[rows, :]
         for i in range(4, 8):
             total = total + rb[i, rows, :].astype(F32)
@@ -445,6 +442,9 @@
 
     partner1()
     for g in range(group):
+        if g == group // 2:
+            pass1(0)
+            pass1(1)
         parts = []
         for e in range(g * per_group, (g + 1) * per_group):
             rows = pl.ds(e // degree * quarter, quarter)
@@ -454,7 +454,6 @@
         acc[edges(g), :] = base + mm(
             one_hot(proc_lanes[edges(g), :], 0, 2 * m), units(table1, 0, 2)
         )
-    pass1(0)
     turn1()
 
     def proc_unit(u, carry):
@@ -465,7 +464,7 @@
 
     lax.fori_loop(2, 6, proc_unit, 0)
     last1((6, 7, 8))
-    for q in ORDER:
+    for q in range(QUARTERS):
         rows = pl.ds(q * quarter, quarter)
         agg = None
         for g in range(q * degree // per_group, (q + 1) * degree // per_group):
@@ -488,6 +487,7 @@
     partner2()
     pass2(0)
     turn2()
+    pass2(1)
     for b in range(cells // wide):
         rows = cell_block(b)
         far_buf[rows, :] += mm(one_hot(key1_lanes[rows, :], m, m), table2[U_PART])
@@ -520,7 +520,9 @@
             enc_x(side, q).wait_send()
             enc_side(side, q).wait_send()
         enc_p(side).wait_send()
-        enc_c(side).wait_send()
+    for q in range(QUARTERS):
+        enc_cx(q).wait_send()
+    enc_cp().wait_send()
     finish1()
     finish2()
 
@@ -538,7 +540,7 @@
     "w_grid_self",
     "w_grid_agg",
 )
-WEIGHTS = ("w_grid_in",) + SQUARE + ("w_grid_out",)
+WEIGHTS = ("w_grid_in",) + SQUARE + ("mesh_emb", "w_grid_out")
 
 
 def shards(
@@ -578,9 +580,10 @@
     out = pl.pallas_call(
         functools.partial(kernel, n_lat, n_lon, WEIGHTS),
         out_shape=jax.ShapeDtypeStruct((variables, cells), BF16),
-        in_specs=[vmem] * 11 + [any_space] * len(WEIGHTS),
+        in_specs=[vmem] * 10 + [any_space] * len(WEIGHTS),
         out_specs=vmem,
         scratch_shapes=[
+            pltpu.VMEM((m, width), BF16),
             pltpu.VMEM((len(SQUARE), width, width), BF16),
             pltpu.VMEM((variables, width), BF16),
             pltpu.VMEM((variables, width), BF16),
@@ -618,7 +621,6 @@
         ),
     )(
         grid_in.T,
-        mesh_emb,
         enc_dest.T,
         enc_node.T,
         enc_dist.T,

time: 91.1 us -> 85.6 us (0.940)
  Pallas kernels: 88.7 us -> 83.2 us
    pallas_call x1, Pallas kernels: 88.7 us -> 83.2 us  [shards(): pl.pallas_call(functools.partial(kernel, n_lat, n_lon, WEIGHTS), out_shap...]
where the time goes in v3:
time: 85.6 us; the launch traced here: 85.5 us
  Pallas kernels  83.2 us (97%)
  local copies, waits for them, and re-layouts  2.22 us (3%)
    pallas_call x1, Pallas kernels, shards(): pl.pallas_call(functools.partial(kernel, n_lat, n_lon, WEIGHTS), out_shap...  83.2 us
    unnamed x1, local copies, waits for them, and re-layouts  2.22 us

profile of v3, /device:TPU:1, one launch (start us, length us, event | category | flops | bytes accessed | tf_op | source)
XLA Modules:
  0.0 85.5 jit_solution(13954503546773667775)
XLA Ops:
  0.0 83.2 %shard_map.226 = bf16[227,2048]{1,0:T(8,128)(2,1)} custom-call(bf16[227,2048]{1,0:T(8,128)(2,1)} %bitcast.13, s32[2,2048]{1,0:T(2,128)} %bitcast.15, s32[2,2048]{1,0:T(2,128)} %bitcast.16, f32[2,2048]{1,0:T(2,128)} %bitcast.17, f32[2,2048]{1,0:T(2,128)} %bitcast.18, s32[8,512]{1,0:T(8,128)} %bitcast.19, f32[8,512]{1,0:T(8,128)} %bitcast.20, ...), custom_call_target="tpu_custom_call" | custom-call | tf_op jit(solution)/shard_map/pallas_call | solution.py:580
  83.3 2.2 %copy.26 = bf16[2048,227]{0,1:T(8,128)(2,1)} copy(bf16[2048,227]{0,1:T(8,128)(2,1)} %bitcast.12) | data formatting | bytes 1859584

commit v4 on v3

--- a/solution.py
+++ b/solution.py
@@ -179,15 +179,6 @@
     cell_keys[2:4, :] = enc_d[...]
     cell_keys[4:6, :] = dec_d[...]
     cell_cols[...] = jnp.transpose(cell_keys[...])
-    mesh_key = gather_key(src[...] >> shift, src[...] & (m - 1)).astype(F32)
-    mesh_key_t = jnp.transpose(mesh_key)
-    proc_cols[...] = jnp.transpose(proc_d[...])
-    for j in range(degree):
-        lanes = jnp.broadcast_to(mesh_key_t[:, j : j + 1], (m, 128)).astype(I32)
-        for q in range(QUARTERS):
-            proc_lanes[pl.ds((q * degree + j) * quarter, quarter), :] = lanes[
-                q * quarter : (q + 1) * quarter
-            ]
 
     fetches["w_grid_in"].wait()
     fetches["w_enc_src"].wait()
@@ -206,8 +197,6 @@
         cols = cell_cols[rows, :]
         for k in range(2):
             msg[k, rows, :] = silu_of_half(e + cols[:, 2 + k : 3 + k] * half_dist).astype(BF16)
-        key0_lanes[rows, :] = jnp.broadcast_to(cols[:, 0:1], (block, 128)).astype(I32)
-        key1_lanes[rows, :] = jnp.broadcast_to(cols[:, 1:2], (block, 128)).astype(I32)
         return carry
 
     lax.fori_loop(0, cells // block, embed, 0)
@@ -276,6 +265,19 @@
             near_buf[rows, :] = recv + cols[:, 4:5] * w_dec_dist[...]
             far_buf[rows, :] = recv + cols[:, 5:6] * w_dec_dist[...]
             u_buf[rows, :] = mm(h, weight("w_grid_self"))
+            key0_lanes[rows, :] = jnp.broadcast_to(cols[:, 0:1], (wide, 128)).astype(I32)
+            key1_lanes[rows, :] = jnp.broadcast_to(cols[:, 1:2], (wide, 128)).astype(I32)
+
+    def mesh_keys():
+        mesh_key = gather_key(src[...] >> shift, src[...] & (m - 1)).astype(F32)
+        mesh_key_t = jnp.transpose(mesh_key)
+        proc_cols[...] = jnp.transpose(proc_d[...])
+        for j in range(degree):
+            lanes = jnp.broadcast_to(mesh_key_t[:, j : j + 1], (m, 128)).astype(I32)
+            for q in range(QUARTERS):
+                proc_lanes[pl.ds((q * degree + j) * quarter, quarter), :] = lanes[
+                    q * quarter : (q + 1) * quarter
+                ]
 
     for upper in range(2):
         for side in range(2):
@@ -310,6 +312,7 @@
 
     lax.fori_loop(2, 8, partial_step, 0)
     relay_sums(1)
+    mesh_keys()
     own_c[...] = scatter(1, 0, 0, m)
     fetches["w_dec_recv"].wait()
     fetches["w_grid_self"].wait()
@@ -317,7 +320,14 @@
     cell_terms(range(0, blocks // 2))
     relay_sums(2)
     cell_terms(range(blocks // 2, blocks))
-    for name in ("mesh_emb", "w_mesh_self", "w_mesh_agg", "w_proc_send"):
+    for name in (
+        "mesh_emb",
+        "w_mesh_self",
+        "w_mesh_agg",
+        "w_proc_send",
+        "w_proc_recv",
+        "w_proc_self",
+    ):
         fetches[name].wait()
     pre[...] = mm(emb[...], weight("w_mesh_self"))
     relay_sums(3)
@@ -389,6 +399,10 @@
             def _():
                 wait_forwarded(CROSS, (0, 1))
 
+            @pl.when(u == 7)
+            def _():
+                wait_forwarded(PARTNER, (2, 3))
+
         def before_partner():
             for q in range(QUARTERS):
                 own(q, PARTNER).wait_recv()
@@ -396,7 +410,8 @@
         def before_last(units):
             if 6 in units:
                 wait_forwarded(CROSS, (0, 1))
-            wait_forwarded(PARTNER, (2, 3))
+            if 7 in units:
+                wait_forwarded(PARTNER, (2, 3))
             wait_forwarded(CROSS, (2, 3))
 
         def finish():
@@ -425,11 +440,11 @@
         mesh_h[rows, :] = h
         table1[U_OWN, rows, :] = mm(h, weight("w_proc_send")).astype(BF16)
         start1(q)
-
-    for name in ("w_proc_recv", "w_proc_self", "w_proc_agg", "w_dec_send"):
+        pre[rows, :] = mm(h, weight("w_proc_recv"))
+        own_c[rows, :] = mm(h, weight("w_proc_self"))
+
+    for name in ("w_proc_agg", "w_dec_send"):
         fetches[name].wait()
-    pre[...] = mm(mesh_h[...], weight("w_proc_recv"))
-    own_c[...] = mm(mesh_h[...], weight("w_proc_self"))
     group = 2 * QUARTERS
     edge_rows = degree * m // group
     per_group = edge_rows // quarter
@@ -499,14 +514,14 @@
             far_buf[rows, :] += mm(one_hot(key1_lanes[rows, :], u * m, m), table2[u])
         return carry
 
-    lax.fori_loop(2, 7, dec_unit, 0)
-    last2((7, 8))
+    lax.fori_loop(2, 8, dec_unit, 0)
+    last2((8,))
     fetches["w_grid_agg"].wait()
     fetches["w_grid_out"].wait()
     for b in range(cells // wide):
         rows = cell_block(b)
         far = far_buf[rows, :] + mm(
-            one_hot(key1_lanes[rows, :], 7 * m, 2 * m), units(table2, 7, 9)
+            one_hot(key1_lanes[rows, :], 8 * m, m), table2[8]
         )
         agg = (near_buf[rows, :] + silu(far)).astype(BF16)
         z = silu(u_buf[rows, :] + mm(agg, weight("w_grid_agg"))).astype(BF16)

time: 85.6 us -> 85.5 us (level)
  no operation moved by 1% of the time
where the time goes in v4:
time: 85.5 us; the launch traced here: 85.3 us
  Pallas kernels  83.1 us (97%)
  local copies, waits for them, and re-layouts  2.22 us (3%)
    pallas_call x1, Pallas kernels, shards(): pl.pallas_call(functools.partial(kernel, n_lat, n_lon, WEIGHTS), out_shap...  83.1 us
    unnamed x1, local copies, waits for them, and re-layouts  2.22 us

profile of v4, /device:TPU:1, one launch (start us, length us, event | category | flops | bytes accessed | tf_op | source)
XLA Modules:
  0.0 85.3 jit_solution(12622092695871351874)
XLA Ops:
  0.0 83.1 %shard_map.226 = bf16[227,2048]{1,0:T(8,128)(2,1)} custom-call(bf16[227,2048]{1,0:T(8,128)(2,1)} %bitcast.13, s32[2,2048]{1,0:T(2,128)} %bitcast.15, s32[2,2048]{1,0:T(2,128)} %bitcast.16, f32[2,2048]{1,0:T(2,128)} %bitcast.17, f32[2,2048]{1,0:T(2,128)} %bitcast.18, s32[8,512]{1,0:T(8,128)} %bitcast.19, f32[8,512]{1,0:T(8,128)} %bitcast.20, ...), custom_call_target="tpu_custom_call" | custom-call | tf_op jit(solution)/shard_map/pallas_call | solution.py:595
  83.1 2.2 %copy.26 = bf16[2048,227]{0,1:T(8,128)(2,1)} copy(bf16[2048,227]{0,1:T(8,128)(2,1)} %bitcast.12) | data formatting | bytes 1859584
